TPU v7x, 256 devices: a whole 4x4x8 slice. The times are simulated.
256 devices in a mesh: case: 8 (over z), gx: 8 (over y, core), gy: 4 (over x).
Axes of the slice: x: 4, y: 4, z: 8, core: 2. Of those that a mesh axis runs over, the one named last changes fastest.
Arguments:
- load: float32 [64, 24, 32, 128], P(('case', 'gx'), 'gy'), parts along dimension 0, may hold values from -4 to 4
- factors: bfloat16 [4, 64, 24, 128, 128], P(None, ('case', 'gx'), 'gy'), parts along dimension 1, may hold values from -6 to 6
- links: int32 [4, 64, 24], P(None, ('case', 'gx'), 'gy'), parts along dimension 1, may hold values from 0 to 1
- shift: float32 [64, 24, 128], P(('case', 'gx'), 'gy'), parts along dimension 0, may hold values from 0.25 to 2.5
Outputs:
- solution: float32 [64, 24, 32, 128], P(('case', 'gx'), 'gy'), parts along dimension 0
- residual: float32 [64, 24, 32, 128], P(('case', 'gx'), 'gy'), parts along dimension 0
There are 8 independent parts, one for each index of `case`. A program takes and returns all parts, laid end to end along the dimension named above; each array names one. Nothing has to cross between parts.
All inputs are finite; a program needn't handle non-finite values.
Results may differ from a plain program's by a relative error of at most 0.008.
Values may be sent and summed in bfloat16 or wider, within the bound.
A program may use at most 64 MiB of HBM per device.

v0:
```python
import functools

import jax
import jax.numpy as jnp
from jax import lax
from jax.experimental import pallas as pl
from jax.experimental.pallas import tpu as pltpu
from jax.sharding import PartitionSpec as P

B = 128
N = 6
R = 32
ITERS = 8
NB = 8
ST = 136
GXN = 8
GYN = 4
PLANE = GXN * GYN
OFFSETS = ((1, 0), (0, 1), (1, 1), (1, -1))
SIDES = ((1, 0), (-1, 0), (0, 1), (0, -1), (1, 1), (1, -1), (-1, 1), (-1, -1))
f32 = jnp.float32
bf16 = jnp.bfloat16


def split3(x):
    a = x.astype(bf16)
    left = x - a.astype(f32)
    b = left.astype(bf16)
    c = (left - b.astype(f32)).astype(bf16)
    return a, b, c


def split2(x):
    a = x.astype(bf16)
    return a, (x - a.astype(f32)).astype(bf16)


def invert(mats):
    lane = lax.broadcasted_iota(jnp.int32, (8, B), 1)
    full_lane = lax.broadcasted_iota(jnp.int32, (B, B), 1)
    full_row = lax.broadcasted_iota(jnp.int32, (B, B), 0)

    def step(b, carry):
        base = b * NB
        rows = [mats[pl.ds(base + i, 8, stride=ST), :] for i in range(NB)]
        e = {}
        for j in range(NB):
            for i in range(j + 1):
                e[i, j] = jnp.sum(jnp.where(lane == base + j, rows[i], 0.0), axis=1, keepdims=True)
        at = lambda i, j: e[min(i, j), max(i, j)]
        for k in range(NB):
            p = 1.0 / e[k, k]
            col = [at(i, k) for i in range(NB)]
            scaled = [c * p for c in col]
            for i in range(NB):
                for j in range(i, NB):
                    if i != k and j != k:
                        e[i, j] = e[i, j] - scaled[i] * col[j]
            for i in range(NB):
                if i != k:
                    e[min(i, k), max(i, k)] = scaled[i]
            e[k, k] = -p
        inside = (lane >= base) & (lane < base + NB)
        sign = jnp.where(lane < base, -1.0, jnp.where(inside, 0.0, 1.0))
        panel = [jnp.where(lane == base + i, 1.0, jnp.where(inside, 0.0, rows[i])) for i in range(NB)]
        cols = []
        for m in range(N):
            cols.append(split3(mats[pl.ds(pl.multiple_of(m * ST + base, 8), 8), :] * sign))
        for j in range(NB):
            total = None
            for i in range(NB):
                term = at(i, j) * panel[i]
                total = term if total is None else total + term
            mats[pl.ds(base + j, 8, stride=ST), :] = -total
        clear = (full_lane >= base) & (full_lane < base + NB) & ((full_row < base) | (full_row >= base + NB))
        for m in range(N):
            r0, r1, r2 = split3(mats[pl.ds(pl.multiple_of(m * ST + base, 8), 8), :])
            c0, c1, c2 = cols[m]
            left = jnp.concatenate([c0, c0, c1, c1, c0, c2], axis=0)
            right = jnp.concatenate([r0, r1, r0, r1, r2, r0], axis=0)
            update = lax.dot_general(left, right, (((0,), (0,)), ((), ())), preferred_element_type=f32)
            span = pl.ds(m * ST, B)
            mats[span, :] = jnp.where(clear, 0.0, mats[span, :]) - update
        return carry

    lax.fori_loop(0, B // NB, step, 0)


def kernel(links, load, factors, shift, x_out, r_out, fac, rem, lm, rlm, mats, wts, pre, ext,
           res, dirn, along, img, dsend, drecv, lsem, fsend, frecv, hsend, hrecv, ssend, srecv):
    case = lax.axis_index("case")
    gx = lax.axis_index("gx")
    gy = lax.axis_index("gy")
    me = gx * GYN + gy

    def device(x, y):
        return (case, x, y)

    def exists(sx, sy):
        ok = None
        for pos, step, count in ((gx, sx, GXN), (gy, sy, GYN)):
            if step == 0:
                continue
            here = (pos + step >= 0) & (pos + step < count)
            ok = here if ok is None else ok & here
        return ok

    mine = pltpu.make_async_copy(factors, fac, lsem.at[0])
    mine.start()
    loaded = pltpu.make_async_copy(load, res, lsem.at[1])
    loaded.start()

    barrier = pltpu.get_barrier_semaphore()
    ext[...] = jnp.zeros_like(ext)
    rem[...] = jnp.zeros_like(rem)
    rlm[...] = jnp.zeros_like(rlm)
    for d in range(4):
        for j in range(N):
            lm[d * N + j : d * N + j + 1, :] = jnp.full((1, B), links[d, 0, j], jnp.int32).astype(f32) * (1.0 / B)

    peers = []
    for k in range(1, PLANE):
        q = lax.rem(me + k, PLANE)
        peers.append(device(q // GYN, lax.rem(q, GYN)))
    for peer in peers:
        pl.semaphore_signal(barrier, inc=1, device_id=peer, device_id_type=pl.DeviceIdType.MESH)
    pl.semaphore_wait(barrier, PLANE - 1)
    mine.wait()

    def remote(src, dst, ss, rs, sx, sy):
        return pltpu.make_async_remote_copy(
            src_ref=src, dst_ref=dst, send_sem=ss, recv_sem=rs,
            device_id=device(gx + sx, gy + sy), device_id_type=pl.DeviceIdType.MESH)

    moves = (
        (1, 0, ((0, 6, 0), (12, 5, 7), (19, 5, 12)), 0),
        (1, 1, ((17, 1, 6),), 1),
        (1, -1, ((18, 1, 17),), 2),
        (0, 1, ((11, 1, 18),), 3),
    )

    def rim_copies(sx, sy, blocks, n):
        copies = []
        for i, (src, count, dst) in enumerate(blocks):
            copies.append(remote(fac.at[pl.ds(src, count)], rem.at[pl.ds(dst, count)],
                                 fsend.at[n * 4 + i], frecv.at[n * 4 + i], sx, sy))
        copies.append(remote(lm, rlm.at[n], fsend.at[n * 4 + 3], frecv.at[n * 4 + 3], sx, sy))
        return copies

    for sx, sy, blocks, n in moves:
        @pl.when(exists(sx, sy))
        def _():
            for copy in rim_copies(sx, sy, blocks, n):
                copy.start()

    def square(block):
        return lax.dot_general(block, block, (((1,), (1,)), ((), ())), preferred_element_type=f32)

    def place(j, slot, s):
        a, b = split2(s)
        wts[j, slot * B : (slot + 1) * B, 0:B] = a
        wts[j, slot * B : (slot + 1) * B, B : 2 * B] = b

    row_id = lax.broadcasted_iota(jnp.int32, (B, B), 0)
    lane_id = lax.broadcasted_iota(jnp.int32, (B, B), 1)
    eye = row_id == lane_id

    def diag_at(j):
        return pl.ds(pl.multiple_of(j * ST, 8), B)

    for m in range(N):
        mats[m * ST : m * ST + B, :] = jnp.where(eye, shift[0, m : m + 1, :], 0.0)
    for m in range(N, 8):
        mats[m * ST : m * ST + B, :] = jnp.where(eye, 1.0, 0.0)

    def own(j, carry):
        total = mats[diag_at(j), :]
        for d in range(4):
            s = square(fac[d * N + j]) * lm[pl.ds(d * N + j, 1), :]
            place(j, d, s)
            total = total + s
            if d == 1:
                after = lax.rem(j + 1, N)
                place(after, 5, s)
                keep = jnp.where(j < N - 1, 1.0, 0.0)
                mats[diag_at(after), :] = mats[diag_at(after), :] + s * keep
        mats[diag_at(j), :] = total
        return carry

    lax.fori_loop(0, N, own, 0)

    for sx, sy, blocks, n in moves:
        @pl.when(exists(-sx, -sy))
        def _():
            for copy in rim_copies(sx, sy, blocks, n):
                copy.wait_recv()

    def theirs(j, carry):
        total = mats[diag_at(j), :]
        s = square(rem[j]) * rlm[0, pl.ds(j, 1), :]
        place(j, 4, s)
        total = total + s
        before = rlm[0, pl.ds(2 * N + jnp.maximum(j - 1, 0), 1), :]
        corner = rlm[1, pl.ds(2 * N + N - 1, 1), :]
        s = square(rem[N + j]) * jnp.where(j == 0, corner, before)
        place(j, 6, s)
        total = total + s
        after = rlm[0, pl.ds(3 * N + jnp.minimum(j + 1, N - 1), 1), :]
        corner = rlm[2, pl.ds(3 * N, 1), :]
        s = square(rem[2 * N + j]) * jnp.where(j == N - 1, corner, after)
        place(j, 7, s)
        mats[diag_at(j), :] = total + s
        return carry

    lax.fori_loop(0, N, theirs, 0)
    s = square(rem[3 * N]) * rlm[3, pl.ds(N + N - 1, 1), :]
    place(0, 5, s)
    mats[0:B, :] = mats[0:B, :] + s

    invert(mats)
    for m in range(N):
        a, b, c = split3(mats[m * ST : m * ST + B, :])
        pre[m, 0:B, 0:B] = a
        pre[m, 0:B, B : 2 * B] = b
        pre[m, B : 2 * B, 0:B] = c
        pre[m, B : 2 * B, B : 2 * B] = jnp.zeros((B, B), bf16)

    for sx, sy, blocks, n in moves:
        @pl.when(exists(sx, sy))
        def _():
            for copy in rim_copies(sx, sy, blocks, n):
                copy.wait_send()

    loaded.wait()
    x_out[...] = jnp.zeros_like(x_out)
    dirn[...] = jnp.zeros_like(dirn)
    along[...] = jnp.zeros_like(along)

    def fold(out):
        small = (out[64:96, 0:B] + out[64:96, B:]) + out[32:64, B:]
        return out[0:32, 0:B] + (out[32:64, 0:B] + (out[0:32, B:] + small))

    def precondition(v, m):
        a, b, c = split3(v)
        left = jnp.concatenate(
            [jnp.concatenate([t, t], axis=1) for t in (a, b, c)], axis=0)
        return fold(jnp.dot(left, pre[m], preferred_element_type=f32))

    def operate(par, j):
        centre = ext[par, 1, 1 + j]
        terms = []
        for sign in (1, -1):
            for sx, sy in OFFSETS:
                terms.append(split3(centre - ext[par, 1 + sign * sx, 1 + j + sign * sy]))
        left = jnp.concatenate(
            [jnp.concatenate([t[i] for t in terms], axis=1) for i in range(3)], axis=0)
        out = fold(jnp.dot(left, wts[j], preferred_element_type=f32))
        return out + shift[0, j : j + 1, :] * centre

    def halo(par):
        for n, (sx, sy) in enumerate(SIDES):
            if sy == 0:
                src = ext.at[par, 1, pl.ds(1, N)]
                dst = ext.at[par, 1 - sx, pl.ds(1, N)]
            else:
                src = ext.at[par, 1, N if sy == 1 else 1]
                dst = ext.at[par, 1 - sx, 0 if sy == 1 else N + 1]
            yield sx, sy, remote(src, dst, hsend.at[n], hrecv.at[par, n], sx, sy)

    lane = lax.broadcasted_iota(jnp.int32, (R, B), 1)
    rhs = lax.broadcasted_iota(jnp.int32, (R, B), 0)

    def iterate(it, carry):
        gamma_old, alpha_old = carry
        par = lax.rem(it, 2)
        for j in range(N):
            ext[par, 1, 1 + j] = precondition(res[0, j], j)
        for sx, sy, copy in halo(par):
            pl.when(exists(sx, sy))(copy.start)
        for sx, sy, copy in halo(par):
            pl.when(exists(-sx, -sy))(copy.wait_recv)
        gsum, dsum = None, None
        for j in range(N):
            w = operate(par, j)
            img[j] = w
            u = ext[par, 1, 1 + j]
            g, d = u * res[0, j], u * w
            gsum = g if gsum is None else gsum + g
            dsum = d if dsum is None else dsum + d
        gcol = jnp.sum(gsum, axis=1, keepdims=True)
        dcol = jnp.sum(dsum, axis=1, keepdims=True)
        spread = jnp.where(lane == rhs, gcol, jnp.where(lane == rhs + R, dcol, 0.0))
        row = jnp.sum(spread, axis=0, keepdims=True)
        dsend[pl.ds(par, 1), :] = row
        drecv[par, pl.ds(me, 1), :] = row

        def contribution(peer):
            return pltpu.make_async_remote_copy(
                src_ref=dsend.at[pl.ds(par, 1)], dst_ref=drecv.at[par, pl.ds(me, 1)],
                send_sem=ssend, recv_sem=srecv.at[par],
                device_id=peer, device_id_type=pl.DeviceIdType.MESH)

        for peer in peers:
            contribution(peer).start()
        everything = drecv.at[par, pl.ds(0, PLANE - 1)]
        pltpu.make_async_copy(everything, everything, srecv.at[par]).wait()
        pltpu.make_async_copy(everything, everything, ssend).wait()
        total = jnp.sum(drecv[par], axis=0, keepdims=True)
        gamma = jnp.sum(jnp.where(lane == rhs, total, 0.0), axis=1, keepdims=True)
        delta = jnp.sum(jnp.where(lane == rhs + R, total, 0.0), axis=1, keepdims=True)
        ratio = jnp.where(it == 0, 0.0, gamma / gamma_old)
        alpha = gamma / (delta - ratio * gamma / alpha_old)
        for j in range(N):
            p = ext[par, 1, 1 + j] + ratio * dirn[j]
            s = img[j] + ratio * along[j]
            dirn[j] = p
            along[j] = s
            x_out[0, j] = x_out[0, j] + alpha * p
            res[0, j] = res[0, j] - alpha * s
        for sx, sy, copy in halo(par):
            pl.when(exists(sx, sy))(copy.wait_send)
        return gamma, alpha

    one = jnp.ones((R, 1), f32)
    lax.fori_loop(0, ITERS, iterate, (one, one))
    r_out[...] = res[...]


def local(load, factors, links, shift):
    vmem = pl.BlockSpec(memory_space=pltpu.VMEM)
    anywhere = pl.BlockSpec(memory_space=pl.ANY)
    field = jax.ShapeDtypeStruct((1, N, R, B), f32)
    return pl.pallas_call(
        kernel,
        out_shape=(field, field),
        in_specs=[pl.BlockSpec(memory_space=pltpu.SMEM), anywhere, anywhere, vmem],
        out_specs=(vmem, vmem),
        scratch_shapes=[
            pltpu.VMEM((4 * N, B, B), bf16),
            pltpu.VMEM((3 * N + 1, B, B), bf16),
            pltpu.VMEM((4 * N, B), f32),
            pltpu.VMEM((4, 4 * N, B), f32),
            pltpu.VMEM((8 * ST, B), f32),
            pltpu.VMEM((N, 8 * B, 2 * B), bf16),
            pltpu.VMEM((N, 2 * B, 2 * B), bf16),
            pltpu.VMEM((2, 3, N + 2, R, B), f32),
            pltpu.VMEM((1, N, R, B), f32),
            pltpu.VMEM((N, R, B), f32),
            pltpu.VMEM((N, R, B), f32),
            pltpu.VMEM((N, R, B), f32),
            pltpu.VMEM((8, B), f32),
            pltpu.VMEM((2, PLANE, B), f32),
            pltpu.SemaphoreType.DMA((2,)),
            pltpu.SemaphoreType.DMA((16,)),
            pltpu.SemaphoreType.DMA((16,)),
            pltpu.SemaphoreType.DMA((8,)),
            pltpu.SemaphoreType.DMA((2, 8)),
            pltpu.SemaphoreType.DMA,
            pltpu.SemaphoreType.DMA((2,)),
        ],
        compiler_params=pltpu.CompilerParams(collective_id=0, has_side_effects=True),
        name="solve",
    )(links, load, factors.reshape(4 * N, B, B), shift)


def solution(mesh):
    placed = (
        P(("case", "gx"), "gy", None, None),
        P(None, ("case", "gx"), "gy", None, None),
        P(None, ("case", "gx"), "gy"),
        P(("case", "gx"), "gy", None),
    )
    return jax.shard_map(
        local,
        mesh=mesh,
        in_specs=placed,
        out_specs=(P(("case", "gx"), "gy", None, None), P(("case", "gx"), "gy", None, None)),
        check_vma=False,
    )
```

profile of v0, /device:TPU:1, one launch (start us, length us, event | category | flops | bytes accessed | tf_op | source)
XLA Modules:
  0.0 112.5 jit_solution(2758428608026379587)
XLA Ops:
  0.6 1.3 %copy.6.shift = f32[1,6,128]{2,1,0:T(8,128)} copy(f32[1,6,128]{2,0,1:T(1,128)} %param.7) | data formatting | bytes 6144 | tf_op args[3]
  1.9 108.4 %solve.1 = (f32[1,6,32,128]{3,2,1,0:T(8,128)}, f32[1,6,32,128]{3,2,1,0:T(8,128)}) custom-call(s32[4,1,6]{2,1,0:T(1,128)} %links.1, f32[1,6,32,128]{3,2,1,0:T(8,128)} %load.1, bf16[24,128,128]{2,1,0:T(8,128)(2,1)} %bitcast.1, f32[1,6,128]{2,1,0:T(8,128)} %copy.6.shift), custom_call_target="tpu_custom_call" | custom-call | tf_op jit(solution)/shard_map/solve/pallas_call | solution.py:333
  110.3 0.0 copy-start
  110.3 1.6 %copy.9 = f32[1,6,32,128]{3,2,1,0:T(8,128)} copy(f32[1,6,32,128]{3,2,1,0:T(8,128)} %get-tuple-element.4) | data formatting | bytes 196608
  111.9 0.0 copy-done
  111.9 0.6 copy.10
Async XLA Ops:
  110.3 1.6 %copy-start = (f32[1,6,32,128]{3,2,1,0:T(8,128)S(1)}, f32[1,6,32,128]{3,2,1,0:T(8,128)}, u32[]{:S(2)}) copy-start(f32[1,6,32,128]{3,2,1,0:T(8,128)} %get-tuple-element.5) | copy-start | bytes 294916
where the time goes:
time: 113 us
  Pallas kernels  108 us (96%)
  local copies, waits for them, and re-layouts  3.5 us (3%)
    pallas_call x1, Pallas kernels, local(): pl.pallas_call(kernel, out_shape=(field, field), in_specs=[pl.BlockSpec(m...  108 us
    unnamed x5, local copies, waits for them, and re-layouts  3.5 us

commit v1 on v0

--- a/solution.py
+++ b/solution.py
@@ -17,7 +17,7 @@
 GYN = 4
 PLANE = GXN * GYN
 OFFSETS = ((1, 0), (0, 1), (1, 1), (1, -1))
-SIDES = ((1, 0), (-1, 0), (0, 1), (0, -1), (1, 1), (1, -1), (-1, 1), (-1, -1))
+SIDES = ((1, 1), (1, -1), (-1, 1), (-1, -1), (1, 0), (-1, 0), (0, 1), (0, -1))
 f32 = jnp.float32
 bf16 = jnp.bfloat16
 
@@ -87,7 +87,7 @@
 
 
 def kernel(links, load, factors, shift, x_out, r_out, fac, rem, lm, rlm, mats, wts, pre, ext,
-           res, dirn, along, img, dsend, drecv, lsem, fsend, frecv, hsend, hrecv, ssend, srecv):
+           field, push, res, dirn, along, img, dsend, drecv, lsem, fsend, frecv, hsend, hrecv, ssend, srecv):
     case = lax.axis_index("case")
     gx = lax.axis_index("gx")
     gy = lax.axis_index("gy")
@@ -160,6 +160,7 @@
         a, b = split2(s)
         wts[j, slot * B : (slot + 1) * B, 0:B] = a
         wts[j, slot * B : (slot + 1) * B, B : 2 * B] = b
+        return a.astype(f32) + b.astype(f32)
 
     row_id = lax.broadcasted_iota(jnp.int32, (B, B), 0)
     lane_id = lax.broadcasted_iota(jnp.int32, (B, B), 1)
@@ -169,7 +170,7 @@
         return pl.ds(pl.multiple_of(j * ST, 8), B)
 
     for m in range(N):
-        mats[m * ST : m * ST + B, :] = jnp.where(eye, shift[0, m : m + 1, :], 0.0)
+        mats[m * ST : m * ST + B, :] = jnp.where(eye, shift[m], 0.0)
     for m in range(N, 8):
         mats[m * ST : m * ST + B, :] = jnp.where(eye, 1.0, 0.0)
 
@@ -177,7 +178,7 @@
         total = mats[diag_at(j), :]
         for d in range(4):
             s = square(fac[d * N + j]) * lm[pl.ds(d * N + j, 1), :]
-            place(j, d, s)
+            s = place(j, d, s)
             total = total + s
             if d == 1:
                 after = lax.rem(j + 1, N)
@@ -198,28 +199,28 @@
     def theirs(j, carry):
         total = mats[diag_at(j), :]
         s = square(rem[j]) * rlm[0, pl.ds(j, 1), :]
-        place(j, 4, s)
+        s = place(j, 4, s)
         total = total + s
         before = rlm[0, pl.ds(2 * N + jnp.maximum(j - 1, 0), 1), :]
         corner = rlm[1, pl.ds(2 * N + N - 1, 1), :]
         s = square(rem[N + j]) * jnp.where(j == 0, corner, before)
-        place(j, 6, s)
+        s = place(j, 6, s)
         total = total + s
         after = rlm[0, pl.ds(3 * N + jnp.minimum(j + 1, N - 1), 1), :]
         corner = rlm[2, pl.ds(3 * N, 1), :]
         s = square(rem[2 * N + j]) * jnp.where(j == N - 1, corner, after)
-        place(j, 7, s)
+        s = place(j, 7, s)
         mats[diag_at(j), :] = total + s
         return carry
 
     lax.fori_loop(0, N, theirs, 0)
     s = square(rem[3 * N]) * rlm[3, pl.ds(N + N - 1, 1), :]
-    place(0, 5, s)
+    s = place(0, 5, s)
     mats[0:B, :] = mats[0:B, :] + s
 
     invert(mats)
     for m in range(N):
-        a, b, c = split3(mats[m * ST : m * ST + B, :])
+        a, b, c = split3(mats[m * ST : m * ST + B, :].T)
         pre[m, 0:B, 0:B] = a
         pre[m, 0:B, B : 2 * B] = b
         pre[m, B : 2 * B, 0:B] = c
@@ -235,6 +236,7 @@
     x_out[...] = jnp.zeros_like(x_out)
     dirn[...] = jnp.zeros_like(dirn)
     along[...] = jnp.zeros_like(along)
+    push[...] = jnp.zeros_like(push)
 
     def fold(out):
         small = (out[64:96, 0:B] + out[64:96, B:]) + out[32:64, B:]
@@ -246,16 +248,16 @@
             [jnp.concatenate([t, t], axis=1) for t in (a, b, c)], axis=0)
         return fold(jnp.dot(left, pre[m], preferred_element_type=f32))
 
-    def operate(par, j):
-        centre = ext[par, 1, 1 + j]
+    def operate(j):
+        centre = field[1, 1 + j]
         terms = []
         for sign in (1, -1):
             for sx, sy in OFFSETS:
-                terms.append(split3(centre - ext[par, 1 + sign * sx, 1 + j + sign * sy]))
+                terms.append(split3(centre - field[1 + sign * sx, 1 + j + sign * sy]))
         left = jnp.concatenate(
             [jnp.concatenate([t[i] for t in terms], axis=1) for i in range(3)], axis=0)
         out = fold(jnp.dot(left, wts[j], preferred_element_type=f32))
-        return out + shift[0, j : j + 1, :] * centre
+        return out + shift[j] * centre
 
     def halo(par):
         for n, (sx, sy) in enumerate(SIDES):
@@ -267,23 +269,33 @@
                 dst = ext.at[par, 1 - sx, 0 if sy == 1 else N + 1]
             yield sx, sy, remote(src, dst, hsend.at[n], hrecv.at[par, n], sx, sy)
 
+    def halo_start(par):
+        for sx, sy, copy in halo(par):
+            pl.when(exists(sx, sy))(copy.start)
+
+    def halo_wait(par):
+        for sx, sy, copy in halo(par):
+            pl.when(exists(-sx, -sy))(copy.wait_recv)
+
+    def halo_sent(par):
+        for sx, sy, copy in halo(par):
+            pl.when(exists(sx, sy))(copy.wait_send)
+
     lane = lax.broadcasted_iota(jnp.int32, (R, B), 1)
     rhs = lax.broadcasted_iota(jnp.int32, (R, B), 0)
 
-    def iterate(it, carry):
-        gamma_old, alpha_old = carry
-        par = lax.rem(it, 2)
-        for j in range(N):
-            ext[par, 1, 1 + j] = precondition(res[0, j], j)
-        for sx, sy, copy in halo(par):
-            pl.when(exists(sx, sy))(copy.start)
-        for sx, sy, copy in halo(par):
-            pl.when(exists(-sx, -sy))(copy.wait_recv)
+    def contribution(par, peer):
+        return pltpu.make_async_remote_copy(
+            src_ref=dsend.at[pl.ds(par, 1)], dst_ref=drecv.at[par, pl.ds(me, 1)],
+            send_sem=ssend, recv_sem=srecv.at[par],
+            device_id=peer, device_id_type=pl.DeviceIdType.MESH)
+
+    def products(par):
         gsum, dsum = None, None
         for j in range(N):
-            w = operate(par, j)
+            w = operate(j)
             img[j] = w
-            u = ext[par, 1, 1 + j]
+            u = field[1, 1 + j]
             g, d = u * res[0, j], u * w
             gsum = g if gsum is None else gsum + g
             dsum = d if dsum is None else dsum + d
@@ -293,37 +305,58 @@
         row = jnp.sum(spread, axis=0, keepdims=True)
         dsend[pl.ds(par, 1), :] = row
         drecv[par, pl.ds(me, 1), :] = row
-
-        def contribution(peer):
-            return pltpu.make_async_remote_copy(
-                src_ref=dsend.at[pl.ds(par, 1)], dst_ref=drecv.at[par, pl.ds(me, 1)],
-                send_sem=ssend, recv_sem=srecv.at[par],
-                device_id=peer, device_id_type=pl.DeviceIdType.MESH)
-
         for peer in peers:
-            contribution(peer).start()
+            contribution(par, peer).start()
+
+    def totals(par, first, gamma_old, alpha_old):
         everything = drecv.at[par, pl.ds(0, PLANE - 1)]
         pltpu.make_async_copy(everything, everything, srecv.at[par]).wait()
         pltpu.make_async_copy(everything, everything, ssend).wait()
         total = jnp.sum(drecv[par], axis=0, keepdims=True)
         gamma = jnp.sum(jnp.where(lane == rhs, total, 0.0), axis=1, keepdims=True)
         delta = jnp.sum(jnp.where(lane == rhs + R, total, 0.0), axis=1, keepdims=True)
-        ratio = jnp.where(it == 0, 0.0, gamma / gamma_old)
+        ratio = jnp.where(first, 0.0, gamma / gamma_old)
         alpha = gamma / (delta - ratio * gamma / alpha_old)
+        return gamma, ratio, alpha
+
+    def advance(j, ratio, alpha):
+        p = field[1, 1 + j] + ratio * dirn[j]
+        s = img[j] + ratio * along[j]
+        return p, s, x_out[0, j] + alpha * p, res[0, j] - alpha * s
+
+    for j in range(N):
+        ext[1, 1, 1 + j] = precondition(res[0, j], j)
+    halo_start(1)
+    halo_wait(1)
+    field[...] = ext[1]
+    halo_sent(1)
+
+    def iterate(it, carry):
+        gamma_old, alpha_old = carry
+        par = lax.rem(it, 2)
+        products(par)
         for j in range(N):
-            p = ext[par, 1, 1 + j] + ratio * dirn[j]
-            s = img[j] + ratio * along[j]
-            dirn[j] = p
-            along[j] = s
-            x_out[0, j] = x_out[0, j] + alpha * p
-            res[0, j] = res[0, j] - alpha * s
-        for sx, sy, copy in halo(par):
-            pl.when(exists(sx, sy))(copy.wait_send)
+            ext[par, 1, 1 + j] = precondition(img[j], j)
+        halo_start(par)
+        gamma, ratio, alpha = totals(par, it == 0, gamma_old, alpha_old)
+        for j in range(N):
+            dirn[j], along[j], x_out[0, j], res[0, j] = advance(j, ratio, alpha)
+        halo_wait(par)
+        for a in range(3):
+            for c in range(N + 2):
+                q = ext[par, a, c] + ratio * push[a, c]
+                push[a, c] = q
+                field[a, c] = field[a, c] - alpha * q
+        halo_sent(par)
         return gamma, alpha
 
     one = jnp.ones((R, 1), f32)
-    lax.fori_loop(0, ITERS, iterate, (one, one))
-    r_out[...] = res[...]
+    gamma_old, alpha_old = lax.fori_loop(0, ITERS - 1, iterate, (one, one))
+    last = (ITERS - 1) % 2
+    products(last)
+    gamma, ratio, alpha = totals(last, ITERS == 1, gamma_old, alpha_old)
+    for j in range(N):
+        _, _, x_out[0, j], r_out[0, j] = advance(j, ratio, alpha)
 
 
 def local(load, factors, links, shift):
@@ -344,6 +377,8 @@
             pltpu.VMEM((N, 8 * B, 2 * B), bf16),
             pltpu.VMEM((N, 2 * B, 2 * B), bf16),
             pltpu.VMEM((2, 3, N + 2, R, B), f32),
+            pltpu.VMEM((3, N + 2, R, B), f32),
+            pltpu.VMEM((3, N + 2, R, B), f32),
             pltpu.VMEM((1, N, R, B), f32),
             pltpu.VMEM((N, R, B), f32),
             pltpu.VMEM((N, R, B), f32),
@@ -360,7 +395,7 @@
         ],
         compiler_params=pltpu.CompilerParams(collective_id=0, has_side_effects=True),
         name="solve",
-    )(links, load, factors.reshape(4 * N, B, B), shift)
+    )(links, load, factors.reshape(4 * N, B, B), shift.reshape(N, 1, B))
 
 
 def solution(mesh):

time: 113 us -> 87.3 us (0.77)
  Pallas kernels: 108 us -> 84.3 us
  local copies, waits for them, and re-layouts: 3.5 us -> 2.22 us
    pallas_call x1, Pallas kernels: 108 us -> 84.3 us  [local(): pl.pallas_call(kernel, out_shape=(field, field), in_specs=[pl.BlockSpec(m...]
    unnamed x5 -> x4, local copies, waits for them, and re-layouts: 3.5 us -> 2.22 us
where the time goes in v1:
time: 87.3 us; the launch traced here: 87.2 us
  Pallas kernels  84.3 us (97%)
  local copies, waits for them, and re-layouts  2.22 us (3%)
    pallas_call x1, Pallas kernels, local(): pl.pallas_call(kernel, out_shape=(field, field), in_specs=[pl.BlockSpec(m...  84.3 us
    unnamed x4, local copies, waits for them, and re-layouts  2.22 us

profile of v1, /device:TPU:1, one launch (start us, length us, event | category | flops | bytes accessed | tf_op | source)
XLA Modules:
  0.0 87.2 jit_solution(1897883671377311918)
XLA Ops:
  0.6 84.3 %solve.1 = (f32[1,6,32,128]{3,2,1,0:T(8,128)}, f32[1,6,32,128]{3,2,1,0:T(8,128)}) custom-call(s32[4,1,6]{2,1,0:T(1,128)} %links.1, f32[1,6,32,128]{3,2,1,0:T(8,128)} %load.1, bf16[24,128,128]{2,1,0:T(8,128)(2,1)} %bitcast.2, f32[6,1,128]{2,1,0:T(1,128)} %bitcast.3), custom_call_target="tpu_custom_call" | custom-call | tf_op jit(solution)/shard_map/solve/pallas_call | solution.py:366
  85.0 0.0 copy-start
  85.0 1.6 %copy.8 = f32[1,6,32,128]{3,2,1,0:T(8,128)} copy(f32[1,6,32,128]{3,2,1,0:T(8,128)} %get-tuple-element.4) | data formatting | bytes 196608
  86.6 0.0 copy-done
  86.6 0.6 copy.9
Async XLA Ops:
  85.0 1.6 %copy-start = (f32[1,6,32,128]{3,2,1,0:T(8,128)S(1)}, f32[1,6,32,128]{3,2,1,0:T(8,128)}, u32[]{:S(2)}) copy-start(f32[1,6,32,128]{3,2,1,0:T(8,128)} %get-tuple-element.5) | copy-start | bytes 294916

commit v2 on v1

--- a/solution.py
+++ b/solution.py
@@ -35,14 +35,17 @@
     return a, (x - a.astype(f32)).astype(bf16)
 
 
-def invert(mats):
+def invert(mats, rpan):
     lane = lax.broadcasted_iota(jnp.int32, (8, B), 1)
-    full_lane = lax.broadcasted_iota(jnp.int32, (B, B), 1)
-    full_row = lax.broadcasted_iota(jnp.int32, (B, B), 0)
-
     def step(b, carry):
         base = b * NB
         rows = [mats[pl.ds(base + i, 8, stride=ST), :] for i in range(NB)]
+        inside = (lane >= base) & (lane < base + NB)
+        sign = jnp.where(lane < base, -1.0, jnp.where(inside, 0.0, 1.0))
+        cols = []
+        for m in range(N):
+            c0, c1, c2 = split3(mats[pl.ds(pl.multiple_of(m * ST + base, 8), 8), :] * sign)
+            cols.append(jnp.concatenate([c0, c0, c1, c1, c0, c2], axis=0))
         e = {}
         for j in range(NB):
             for i in range(j + 1):
@@ -60,33 +63,28 @@
                 if i != k:
                     e[min(i, k), max(i, k)] = scaled[i]
             e[k, k] = -p
-        inside = (lane >= base) & (lane < base + NB)
-        sign = jnp.where(lane < base, -1.0, jnp.where(inside, 0.0, 1.0))
         panel = [jnp.where(lane == base + i, 1.0, jnp.where(inside, 0.0, rows[i])) for i in range(NB)]
-        cols = []
-        for m in range(N):
-            cols.append(split3(mats[pl.ds(pl.multiple_of(m * ST + base, 8), 8), :] * sign))
         for j in range(NB):
             total = None
             for i in range(NB):
                 term = at(i, j) * panel[i]
                 total = term if total is None else total + term
-            mats[pl.ds(base + j, 8, stride=ST), :] = -total
-        clear = (full_lane >= base) & (full_lane < base + NB) & ((full_row < base) | (full_row >= base + NB))
+            rpan[pl.ds(j, 8, stride=NB), :] = -total
+        ups = []
         for m in range(N):
-            r0, r1, r2 = split3(mats[pl.ds(pl.multiple_of(m * ST + base, 8), 8), :])
-            c0, c1, c2 = cols[m]
-            left = jnp.concatenate([c0, c0, c1, c1, c0, c2], axis=0)
+            r0, r1, r2 = split3(rpan[m * NB : (m + 1) * NB, :])
             right = jnp.concatenate([r0, r1, r0, r1, r2, r0], axis=0)
-            update = lax.dot_general(left, right, (((0,), (0,)), ((), ())), preferred_element_type=f32)
-            span = pl.ds(m * ST, B)
-            mats[span, :] = jnp.where(clear, 0.0, mats[span, :]) - update
+            ups.append(lax.dot_general(cols[m], right, (((0,), (0,)), ((), ())), preferred_element_type=f32))
+        new = [jnp.where(inside[0:1, :], 0.0, mats[m * ST : m * ST + B, :]) - ups[m] for m in range(N)]
+        for m in range(N):
+            mats[m * ST : m * ST + B, :] = new[m]
+        for m in range(N):
+            mats[pl.ds(pl.multiple_of(m * ST + base, 8), 8), :] = rpan[m * NB : (m + 1) * NB, :]
         return carry
-
     lax.fori_loop(0, B // NB, step, 0)
 
 
-def kernel(links, load, factors, shift, x_out, r_out, fac, rem, lm, rlm, mats, wts, pre, ext,
+def kernel(links_in, load, factors, shift_in, x_out, r_out, links, shift, fac, rem, lm, rlm, mats, rpan, dpan, wts, pre, ext,
            field, push, res, dirn, along, img, dsend, drecv, lsem, fsend, frecv, hsend, hrecv, ssend, srecv):
     case = lax.axis_index("case")
     gx = lax.axis_index("gx")
@@ -105,27 +103,32 @@
             ok = here if ok is None else ok & here
         return ok
 
-    mine = pltpu.make_async_copy(factors, fac, lsem.at[0])
-    mine.start()
-    loaded = pltpu.make_async_copy(load, res, lsem.at[1])
-    loaded.start()
-
     barrier = pltpu.get_barrier_semaphore()
+    peers = []
+    for a in (4, 3, 5, 2, 6, 1, 7, 0):
+        for c in (2, 1, 3, 0):
+            if a or c:
+                peers.append(device(lax.rem(gx + a, GXN), lax.rem(gy + c, GYN)))
+
     ext[...] = jnp.zeros_like(ext)
     rem[...] = jnp.zeros_like(rem)
     rlm[...] = jnp.zeros_like(rlm)
+    for peer in peers:
+        pl.semaphore_signal(barrier, inc=1, device_id=peer, device_id_type=pl.DeviceIdType.MESH)
+    copies = [
+        pltpu.make_async_copy(factors, fac, lsem.at[0]),
+        pltpu.make_async_copy(links_in, links, lsem.at[1]),
+        pltpu.make_async_copy(shift_in, shift, lsem.at[2]),
+        pltpu.make_async_copy(load, res, lsem.at[3]),
+    ]
+    for copy in copies:
+        copy.start()
+    copies[1].wait()
     for d in range(4):
         for j in range(N):
             lm[d * N + j : d * N + j + 1, :] = jnp.full((1, B), links[d, 0, j], jnp.int32).astype(f32) * (1.0 / B)
-
-    peers = []
-    for k in range(1, PLANE):
-        q = lax.rem(me + k, PLANE)
-        peers.append(device(q // GYN, lax.rem(q, GYN)))
-    for peer in peers:
-        pl.semaphore_signal(barrier, inc=1, device_id=peer, device_id_type=pl.DeviceIdType.MESH)
+    copies[0].wait()
     pl.semaphore_wait(barrier, PLANE - 1)
-    mine.wait()
 
     def remote(src, dst, ss, rs, sx, sy):
         return pltpu.make_async_remote_copy(
@@ -133,25 +136,25 @@
             device_id=device(gx + sx, gy + sy), device_id_type=pl.DeviceIdType.MESH)
 
     moves = (
-        (1, 0, ((0, 6, 0), (12, 5, 7), (19, 5, 12)), 0),
         (1, 1, ((17, 1, 6),), 1),
         (1, -1, ((18, 1, 17),), 2),
         (0, 1, ((11, 1, 18),), 3),
+        (1, 0, ((0, 6, 0), (12, 5, 7), (19, 5, 12)), 0),
     )
 
-    def rim_copies(sx, sy, blocks, n):
-        copies = []
+    def rim_copies(sx, sy, blocks, n, low=0, high=4):
+        parts = [(lm, rlm.at[n], n * 4 + 3)]
         for i, (src, count, dst) in enumerate(blocks):
-            copies.append(remote(fac.at[pl.ds(src, count)], rem.at[pl.ds(dst, count)],
-                                 fsend.at[n * 4 + i], frecv.at[n * 4 + i], sx, sy))
-        copies.append(remote(lm, rlm.at[n], fsend.at[n * 4 + 3], frecv.at[n * 4 + 3], sx, sy))
-        return copies
+            parts.append((fac.at[pl.ds(src, count)], rem.at[pl.ds(dst, count)], n * 4 + i))
+        return [remote(src, dst, fsend.at[i], frecv.at[i], sx, sy) for src, dst, i in parts[low:high]]
 
     for sx, sy, blocks, n in moves:
         @pl.when(exists(sx, sy))
         def _():
             for copy in rim_copies(sx, sy, blocks, n):
                 copy.start()
+
+    copies[2].wait()
 
     def square(block):
         return lax.dot_general(block, block, (((1,), (1,)), ((), ())), preferred_element_type=f32)
@@ -190,37 +193,60 @@
 
     lax.fori_loop(0, N, own, 0)
 
-    for sx, sy, blocks, n in moves:
+    def arrived(n, low, high):
+        sx, sy, blocks, _ = moves[n]
         @pl.when(exists(-sx, -sy))
         def _():
-            for copy in rim_copies(sx, sy, blocks, n):
+            for copy in rim_copies(*moves[n], low, high):
                 copy.wait_recv()
 
-    def theirs(j, carry):
-        total = mats[diag_at(j), :]
-        s = square(rem[j]) * rlm[0, pl.ds(j, 1), :]
-        s = place(j, 4, s)
-        total = total + s
-        before = rlm[0, pl.ds(2 * N + jnp.maximum(j - 1, 0), 1), :]
-        corner = rlm[1, pl.ds(2 * N + N - 1, 1), :]
-        s = square(rem[N + j]) * jnp.where(j == 0, corner, before)
-        s = place(j, 6, s)
-        total = total + s
-        after = rlm[0, pl.ds(3 * N + jnp.minimum(j + 1, N - 1), 1), :]
-        corner = rlm[2, pl.ds(3 * N, 1), :]
-        s = square(rem[2 * N + j]) * jnp.where(j == N - 1, corner, after)
-        s = place(j, 7, s)
-        mats[diag_at(j), :] = total + s
-        return carry
-
-    lax.fori_loop(0, N, theirs, 0)
-    s = square(rem[3 * N]) * rlm[3, pl.ds(N + N - 1, 1), :]
-    s = place(0, 5, s)
-    mats[0:B, :] = mats[0:B, :] + s
-
-    invert(mats)
+    def term(j, slot, block, scale):
+        return j, place(j, slot, square(rem[block]) * scale)
+
+    def collect(terms):
+        for j, s in terms:
+            mats[j * ST : j * ST + B, :] = mats[j * ST : j * ST + B, :] + s
+
+    arrived(0, 0, 2)
+    arrived(1, 0, 2)
+    arrived(2, 0, 2)
+    collect([
+        term(0, 6, N, rlm[1, 3 * N - 1 : 3 * N, :]),
+        term(N - 1, 7, 3 * N - 1, rlm[2, 3 * N : 3 * N + 1, :]),
+        term(0, 5, 3 * N, rlm[3, 2 * N - 1 : 2 * N, :]),
+    ])
+    arrived(3, 0, 2)
+    collect([term(j, 4, j, rlm[0, j : j + 1, :]) for j in range(N)])
+    arrived(3, 2, 3)
+    collect([term(j, 6, N + j, rlm[0, 2 * N + j - 1 : 2 * N + j, :]) for j in range(1, N)])
+    arrived(3, 3, 4)
+    collect([term(j, 7, 2 * N + j, rlm[0, 3 * N + j + 1 : 3 * N + j + 2, :]) for j in range(N - 1)])
+
     for m in range(N):
-        a, b, c = split3(mats[m * ST : m * ST + B, :].T)
+        a, b, c = split3(mats[m * ST : m * ST + B, :])
+        dpan[m, 0:B, 0:B] = a
+        dpan[m, 0:B, B : 2 * B] = b
+        dpan[m, B : 2 * B, 0:B] = c
+        dpan[m, B : 2 * B, B : 2 * B] = jnp.zeros((B, B), bf16)
+    invert(mats, rpan)
+
+    def pairs(terms):
+        return jnp.concatenate([jnp.concatenate([t, t], axis=1) for t in terms], axis=0)
+
+    def fold(out, h):
+        small = (out[2 * h :, 0:B] + out[2 * h :, B:]) + out[h : 2 * h, B:]
+        return out[0:h, 0:B] + (out[h : 2 * h, 0:B] + (out[0:h, B:] + small))
+
+    better = []
+    for m in range(N):
+        inv = mats[m * ST : m * ST + B, :]
+        terms = split3(inv)
+        product = fold(jnp.dot(pairs(terms), dpan[m], preferred_element_type=f32), B)
+        error = (jnp.where(eye, 1.0, 0.0) - product).astype(bf16)
+        fix = jnp.dot(error, jnp.concatenate(terms[0:2], axis=1), preferred_element_type=f32)
+        better.append(inv + (fix[:, 0:B] + fix[:, B:]))
+    for m in range(N):
+        a, b, c = split3(better[m])
         pre[m, 0:B, 0:B] = a
         pre[m, 0:B, B : 2 * B] = b
         pre[m, B : 2 * B, 0:B] = c
@@ -232,21 +258,14 @@
             for copy in rim_copies(sx, sy, blocks, n):
                 copy.wait_send()
 
-    loaded.wait()
+    copies[3].wait()
     x_out[...] = jnp.zeros_like(x_out)
     dirn[...] = jnp.zeros_like(dirn)
     along[...] = jnp.zeros_like(along)
     push[...] = jnp.zeros_like(push)
 
-    def fold(out):
-        small = (out[64:96, 0:B] + out[64:96, B:]) + out[32:64, B:]
-        return out[0:32, 0:B] + (out[32:64, 0:B] + (out[0:32, B:] + small))
-
     def precondition(v, m):
-        a, b, c = split3(v)
-        left = jnp.concatenate(
-            [jnp.concatenate([t, t], axis=1) for t in (a, b, c)], axis=0)
-        return fold(jnp.dot(left, pre[m], preferred_element_type=f32))
+        return fold(jnp.dot(pairs(split3(v)), pre[m], preferred_element_type=f32), R)
 
     def operate(j):
         centre = field[1, 1 + j]
@@ -256,7 +275,7 @@
                 terms.append(split3(centre - field[1 + sign * sx, 1 + j + sign * sy]))
         left = jnp.concatenate(
             [jnp.concatenate([t[i] for t in terms], axis=1) for i in range(3)], axis=0)
-        out = fold(jnp.dot(left, wts[j], preferred_element_type=f32))
+        out = fold(jnp.dot(left, wts[j], preferred_element_type=f32), R)
         return out + shift[j] * centre
 
     def halo(par):
@@ -361,19 +380,23 @@
 
 def local(load, factors, links, shift):
     vmem = pl.BlockSpec(memory_space=pltpu.VMEM)
-    anywhere = pl.BlockSpec(memory_space=pl.ANY)
+    hbm = pl.BlockSpec(memory_space=pltpu.HBM)
     field = jax.ShapeDtypeStruct((1, N, R, B), f32)
     return pl.pallas_call(
         kernel,
         out_shape=(field, field),
-        in_specs=[pl.BlockSpec(memory_space=pltpu.SMEM), anywhere, anywhere, vmem],
+        in_specs=[hbm] * 4,
         out_specs=(vmem, vmem),
         scratch_shapes=[
+            pltpu.SMEM((4, 1, N), jnp.int32),
+            pltpu.VMEM((N, 1, B), f32),
             pltpu.VMEM((4 * N, B, B), bf16),
             pltpu.VMEM((3 * N + 1, B, B), bf16),
             pltpu.VMEM((4 * N, B), f32),
             pltpu.VMEM((4, 4 * N, B), f32),
             pltpu.VMEM((8 * ST, B), f32),
+            pltpu.VMEM((8 * NB, B), f32),
+            pltpu.VMEM((N, 2 * B, 2 * B), bf16),
             pltpu.VMEM((N, 8 * B, 2 * B), bf16),
             pltpu.VMEM((N, 2 * B, 2 * B), bf16),
             pltpu.VMEM((2, 3, N + 2, R, B), f32),
@@ -385,7 +408,7 @@
             pltpu.VMEM((N, R, B), f32),
             pltpu.VMEM((8, B), f32),
             pltpu.VMEM((2, PLANE, B), f32),
-            pltpu.SemaphoreType.DMA((2,)),
+            pltpu.SemaphoreType.DMA((4,)),
             pltpu.SemaphoreType.DMA((16,)),
             pltpu.SemaphoreType.DMA((16,)),
             pltpu.SemaphoreType.DMA((8,)),

time: 87.3 us -> 74.9 us (0.86)
  Pallas kernels: 84.3 us -> 71.9 us
    pallas_call x1, Pallas kernels: 84.3 us -> 71.9 us  [local(): pl.pallas_call(kernel, out_shape=(field, field), in_specs=[hbm] * 4, out_...]
where the time goes in v2:
time: 74.9 us; the launch traced here: 74.7 us
  Pallas kernels  71.9 us (96%)
  local copies, waits for them, and re-layouts  2.22 us (3%)
    pallas_call x1, Pallas kernels, local(): pl.pallas_call(kernel, out_shape=(field, field), in_specs=[hbm] * 4, out_...  71.9 us
    unnamed x4, local copies, waits for them, and re-layouts  2.22 us

profile of v2, /device:TPU:1, one launch (start us, length us, event | category | flops | bytes accessed | tf_op | source)
XLA Modules:
  0.0 74.7 jit_solution(14658723871054323323)
XLA Ops:
  0.6 71.9 %solve.1 = (f32[1,6,32,128]{3,2,1,0:T(8,128)}, f32[1,6,32,128]{3,2,1,0:T(8,128)}) custom-call(s32[4,1,6]{2,1,0:T(1,128)} %links_in.1, f32[1,6,32,128]{3,2,1,0:T(8,128)} %load.1, bf16[24,128,128]{2,1,0:T(8,128)(2,1)} %bitcast.2, f32[6,1,128]{2,1,0:T(1,128)} %bitcast.3), custom_call_target="tpu_custom_call" | custom-call | tf_op jit(solution)/shard_map/solve/pallas_call | solution.py:385
  72.5 0.0 copy-start
  72.5 1.6 %copy.8 = f32[1,6,32,128]{3,2,1,0:T(8,128)} copy(f32[1,6,32,128]{3,2,1,0:T(8,128)} %get-tuple-element.4) | data formatting | bytes 196608
  74.1 0.0 copy-done
  74.1 0.6 copy.9
Async XLA Ops:
  72.5 1.6 %copy-start = (f32[1,6,32,128]{3,2,1,0:T(8,128)S(1)}, f32[1,6,32,128]{3,2,1,0:T(8,128)}, u32[]{:S(2)}) copy-start(f32[1,6,32,128]{3,2,1,0:T(8,128)} %get-tuple-element.5) | copy-start | bytes 294916

commit v3 on v2

--- a/solution.py
+++ b/solution.py
@@ -85,7 +85,7 @@
 
 
 def kernel(links_in, load, factors, shift_in, x_out, r_out, links, shift, fac, rem, lm, rlm, mats, rpan, dpan, wts, pre, ext,
-           field, push, res, dirn, along, img, dsend, drecv, lsem, fsend, frecv, hsend, hrecv, ssend, srecv):
+           pre_u, push, qdir, zdir, res, dirn, along, img, dsend, drecv, lsem, fsend, frecv, hsend, hrecv, ssend, srecv):
     case = lax.axis_index("case")
     gx = lax.axis_index("gx")
     gy = lax.axis_index("gy")
@@ -262,17 +262,18 @@
     x_out[...] = jnp.zeros_like(x_out)
     dirn[...] = jnp.zeros_like(dirn)
     along[...] = jnp.zeros_like(along)
-    push[...] = jnp.zeros_like(push)
+    qdir[...] = jnp.zeros_like(qdir)
+    zdir[...] = jnp.zeros_like(zdir)
 
     def precondition(v, m):
         return fold(jnp.dot(pairs(split3(v)), pre[m], preferred_element_type=f32), R)
 
-    def operate(j):
-        centre = field[1, 1 + j]
+    def operate(par, j):
+        centre = ext[par, 1, 1 + j]
         terms = []
         for sign in (1, -1):
             for sx, sy in OFFSETS:
-                terms.append(split3(centre - field[1 + sign * sx, 1 + j + sign * sy]))
+                terms.append(split3(centre - ext[par, 1 + sign * sx, 1 + j + sign * sy]))
         left = jnp.concatenate(
             [jnp.concatenate([t[i] for t in terms], axis=1) for i in range(3)], axis=0)
         out = fold(jnp.dot(left, wts[j], preferred_element_type=f32), R)
@@ -309,13 +310,10 @@
             send_sem=ssend, recv_sem=srecv.at[par],
             device_id=peer, device_id_type=pl.DeviceIdType.MESH)
 
-    def products(par):
+    def products(par, triples):
         gsum, dsum = None, None
-        for j in range(N):
-            w = operate(j)
-            img[j] = w
-            u = field[1, 1 + j]
-            g, d = u * res[0, j], u * w
+        for r, u, w in triples:
+            g, d = u * r, u * w
             gsum = g if gsum is None else gsum + g
             dsum = d if dsum is None else dsum + d
         gcol = jnp.sum(gsum, axis=1, keepdims=True)
@@ -338,44 +336,52 @@
         alpha = gamma / (delta - ratio * gamma / alpha_old)
         return gamma, ratio, alpha
 
-    def advance(j, ratio, alpha):
-        p = field[1, 1 + j] + ratio * dirn[j]
-        s = img[j] + ratio * along[j]
-        return p, s, x_out[0, j] + alpha * p, res[0, j] - alpha * s
-
     for j in range(N):
         ext[1, 1, 1 + j] = precondition(res[0, j], j)
     halo_start(1)
     halo_wait(1)
-    field[...] = ext[1]
+    triples = []
+    for j in range(N):
+        u, w = ext[1, 1, 1 + j], operate(1, j)
+        pre_u[j], img[j] = u, w
+        triples.append((res[0, j], u, w))
+    products(0, triples)
     halo_sent(1)
 
     def iterate(it, carry):
         gamma_old, alpha_old = carry
         par = lax.rem(it, 2)
-        products(par)
         for j in range(N):
             ext[par, 1, 1 + j] = precondition(img[j], j)
         halo_start(par)
+        halo_wait(par)
+        for j in range(N):
+            push[j] = operate(par, j)
         gamma, ratio, alpha = totals(par, it == 0, gamma_old, alpha_old)
+        triples = []
         for j in range(N):
-            dirn[j], along[j], x_out[0, j], res[0, j] = advance(j, ratio, alpha)
-        halo_wait(par)
-        for a in range(3):
-            for c in range(N + 2):
-                q = ext[par, a, c] + ratio * push[a, c]
-                push[a, c] = q
-                field[a, c] = field[a, c] - alpha * q
+            u, w = pre_u[j], img[j]
+            z = push[j] + ratio * zdir[j]
+            q = ext[par, 1, 1 + j] + ratio * qdir[j]
+            s = w + ratio * along[j]
+            p = u + ratio * dirn[j]
+            zdir[j], qdir[j], along[j], dirn[j] = z, q, s, p
+            x_out[0, j] = x_out[0, j] + alpha * p
+            r = res[0, j] - alpha * s
+            u = u - alpha * q
+            w = w - alpha * z
+            res[0, j], pre_u[j], img[j] = r, u, w
+            triples.append((r, u, w))
+        products(1 - par, triples)
         halo_sent(par)
         return gamma, alpha
 
     one = jnp.ones((R, 1), f32)
     gamma_old, alpha_old = lax.fori_loop(0, ITERS - 1, iterate, (one, one))
-    last = (ITERS - 1) % 2
-    products(last)
-    gamma, ratio, alpha = totals(last, ITERS == 1, gamma_old, alpha_old)
+    gamma, ratio, alpha = totals((ITERS - 1) % 2, ITERS == 1, gamma_old, alpha_old)
     for j in range(N):
-        _, _, x_out[0, j], r_out[0, j] = advance(j, ratio, alpha)
+        x_out[0, j] = x_out[0, j] + alpha * (pre_u[j] + ratio * dirn[j])
+        r_out[0, j] = res[0, j] - alpha * (img[j] + ratio * along[j])
 
 
 def local(load, factors, links, shift):
@@ -400,8 +406,10 @@
             pltpu.VMEM((N, 8 * B, 2 * B), bf16),
             pltpu.VMEM((N, 2 * B, 2 * B), bf16),
             pltpu.VMEM((2, 3, N + 2, R, B), f32),
-            pltpu.VMEM((3, N + 2, R, B), f32),
-            pltpu.VMEM((3, N + 2, R, B), f32),
+            pltpu.VMEM((N, R, B), f32),
+            pltpu.VMEM((N, R, B), f32),
+            pltpu.VMEM((N, R, B), f32),
+            pltpu.VMEM((N, R, B), f32),
             pltpu.VMEM((1, N, R, B), f32),
             pltpu.VMEM((N, R, B), f32),
             pltpu.VMEM((N, R, B), f32),
@@ -416,9 +424,9 @@
             pltpu.SemaphoreType.DMA,
             pltpu.SemaphoreType.DMA((2,)),
         ],
-        compiler_params=pltpu.CompilerParams(collective_id=0, has_side_effects=True),
+        compiler_params=pltpu.CompilerParams(collective_id=0, has_side_effects=True, vmem_limit_bytes=24 * 1024 * 1024),
         name="solve",
-    )(links, load, factors.reshape(4 * N, B, B), shift.reshape(N, 1, B))
+    )(*[pltpu.with_memory_space_constraint(t, pltpu.HBM) for t in (links, load, factors.reshape(4 * N, B, B), shift.reshape(N, 1, B))])
 
 
 def solution(mesh):

time: 74.9 us -> 70.6 us (0.943)
  Pallas kernels: 71.9 us -> 68.5 us
  local copies, waits for them, and re-layouts: 2.22 us -> 1.28 us
    pallas_call x1, Pallas kernels: 71.9 us -> 68.5 us  [local(): pl.pallas_call(kernel, out_shape=(field, field), in_specs=[hbm] * 4, out_...]
    unnamed x4 -> x2, local copies, waits for them, and re-layouts: 2.22 us -> 1.28 us
where the time goes in v3:
time: 70.6 us; the launch traced here: 70.5 us
  Pallas kernels  68.5 us (97%)
  local copies, waits for them, and re-layouts  1.28 us (2%)
    pallas_call x1, Pallas kernels, local(): pl.pallas_call(kernel, out_shape=(field, field), in_specs=[hbm] * 4, out_...  68.5 us

profile of v3, /device:TPU:1, one launch (start us, length us, event | category | flops | bytes accessed | tf_op | source)
XLA Modules:
  0.0 70.5 jit_solution(19208617676649937)
XLA Ops:
  0.6 68.5 %solve.1 = (f32[1,6,32,128]{3,2,1,0:T(8,128)S(1)}, f32[1,6,32,128]{3,2,1,0:T(8,128)S(1)}) custom-call(s32[4,1,6]{2,1,0:T(1,128)} %links_in.1, f32[1,6,32,128]{3,2,1,0:T(8,128)} %load.1, bf16[24,128,128]{2,1,0:T(8,128)(2,1)} %bitcast.2, f32[6,1,128]{2,1,0:T(1,128)} %bitcast.3), custom_call_target="tpu_custom_call" | custom-call | tf_op jit(solution)/shard_map/solve/pallas_call | solution.py:391
  69.2 0.6 copy.8
  69.8 0.6 copy.9

commit v4 on v3

--- a/solution.py
+++ b/solution.py
@@ -85,7 +85,7 @@
 
 
 def kernel(links_in, load, factors, shift_in, x_out, r_out, links, shift, fac, rem, lm, rlm, mats, rpan, dpan, wts, pre, ext,
-           pre_u, push, qdir, zdir, res, dirn, along, img, dsend, drecv, lsem, fsend, frecv, hsend, hrecv, ssend, srecv):
+           pre_u, push, qdir, zdir, res, dirn, along, img, dsend, drecv, lsem, fsend, frecv, hsend, hrecv, ssend, srecv, known):
     case = lax.axis_index("case")
     gx = lax.axis_index("gx")
     gy = lax.axis_index("gy")
@@ -113,8 +113,20 @@
     ext[...] = jnp.zeros_like(ext)
     rem[...] = jnp.zeros_like(rem)
     rlm[...] = jnp.zeros_like(rlm)
-    for peer in peers:
+    flip_x = [gx + d - 2 * d * lax.rem(gx // d, 2) for d in (1, 2, 4)]
+    flip_y = [gy + d - 2 * d * lax.rem(gy // d, 2) for d in (1, 2)]
+    partners = [device(x, gy) for x in flip_x] + [device(gx, y) for y in flip_y]
+    greeted = [device(lax.rem(gx + sx + GXN, GXN), lax.rem(gy + sy + GYN, GYN)) for sx, sy in SIDES]
+    greeted += [partners[1], partners[2], partners[4]]
+    for peer in greeted:
         pl.semaphore_signal(barrier, inc=1, device_id=peer, device_id_type=pl.DeviceIdType.MESH)
+
+    def tell(i):
+        pl.semaphore_signal(known.at[i], inc=1, device_id=partners[i], device_id_type=pl.DeviceIdType.MESH)
+
+    def hear(i):
+        pl.semaphore_wait(known.at[i], 1)
+
     copies = [
         pltpu.make_async_copy(factors, fac, lsem.at[0]),
         pltpu.make_async_copy(links_in, links, lsem.at[1]),
@@ -128,7 +140,7 @@
         for j in range(N):
             lm[d * N + j : d * N + j + 1, :] = jnp.full((1, B), links[d, 0, j], jnp.int32).astype(f32) * (1.0 / B)
     copies[0].wait()
-    pl.semaphore_wait(barrier, PLANE - 1)
+    pl.semaphore_wait(barrier, len(greeted))
 
     def remote(src, dst, ss, rs, sx, sy):
         return pltpu.make_async_remote_copy(
@@ -154,6 +166,7 @@
             for copy in rim_copies(sx, sy, blocks, n):
                 copy.start()
 
+    tell(0)
     copies[2].wait()
 
     def square(block):
@@ -192,6 +205,8 @@
         return carry
 
     lax.fori_loop(0, N, own, 0)
+    hear(0)
+    tell(1)
 
     def arrived(n, low, high):
         sx, sy, blocks, _ = moves[n]
@@ -215,10 +230,16 @@
         term(N - 1, 7, 3 * N - 1, rlm[2, 3 * N : 3 * N + 1, :]),
         term(0, 5, 3 * N, rlm[3, 2 * N - 1 : 2 * N, :]),
     ])
+    hear(1)
+    tell(2)
     arrived(3, 0, 2)
     collect([term(j, 4, j, rlm[0, j : j + 1, :]) for j in range(N)])
+    hear(2)
+    tell(3)
     arrived(3, 2, 3)
     collect([term(j, 6, N + j, rlm[0, 2 * N + j - 1 : 2 * N + j, :]) for j in range(1, N)])
+    hear(3)
+    tell(4)
     arrived(3, 3, 4)
     collect([term(j, 7, 2 * N + j, rlm[0, 3 * N + j + 1 : 3 * N + j + 2, :]) for j in range(N - 1)])
 
@@ -229,6 +250,7 @@
         dpan[m, B : 2 * B, 0:B] = c
         dpan[m, B : 2 * B, B : 2 * B] = jnp.zeros((B, B), bf16)
     invert(mats, rpan)
+    hear(4)
 
     def pairs(terms):
         return jnp.concatenate([jnp.concatenate([t, t], axis=1) for t in terms], axis=0)
@@ -423,6 +445,7 @@
             pltpu.SemaphoreType.DMA((2, 8)),
             pltpu.SemaphoreType.DMA,
             pltpu.SemaphoreType.DMA((2,)),
+            pltpu.SemaphoreType.REGULAR((5,)),
         ],
         compiler_params=pltpu.CompilerParams(collective_id=0, has_side_effects=True, vmem_limit_bytes=24 * 1024 * 1024),
         name="solve",

time: 70.6 us -> 69.1 us (0.979)
  Pallas kernels: 68.5 us -> 67.1 us
    pallas_call x1, Pallas kernels: 68.5 us -> 67.1 us  [local(): pl.pallas_call(kernel, out_shape=(field, field), in_specs=[hbm] * 4, out_...]
where the time goes in v4:
time: 69.1 us; the launch traced here: 69 us
  Pallas kernels  67.1 us (97%)
  local copies, waits for them, and re-layouts  1.28 us (2%)
    pallas_call x1, Pallas kernels, local(): pl.pallas_call(kernel, out_shape=(field, field), in_specs=[hbm] * 4, out_...  67.1 us

profile of v4, /device:TPU:1, one launch (start us, length us, event | category | flops | bytes accessed | tf_op | source)
XLA Modules:
  0.0 69.0 jit_solution(9157665737281989359)
XLA Ops:
  0.6 67.1 %solve.1 = (f32[1,6,32,128]{3,2,1,0:T(8,128)S(1)}, f32[1,6,32,128]{3,2,1,0:T(8,128)S(1)}) custom-call(s32[4,1,6]{2,1,0:T(1,128)} %links_in.1, f32[1,6,32,128]{3,2,1,0:T(8,128)} %load.1, bf16[24,128,128]{2,1,0:T(8,128)(2,1)} %bitcast.2, f32[6,1,128]{2,1,0:T(1,128)} %bitcast.3), custom_call_target="tpu_custom_call" | custom-call | tf_op jit(solution)/shard_map/solve/pallas_call | solution.py:413
  67.7 0.6 copy.8
  68.4 0.6 copy.9

commit v5 on v3

--- a/solution.py
+++ b/solution.py
@@ -85,7 +85,8 @@
 
 
 def kernel(links_in, load, factors, shift_in, x_out, r_out, links, shift, fac, rem, lm, rlm, mats, rpan, dpan, wts, pre, ext,
-           pre_u, push, qdir, zdir, res, dirn, along, img, dsend, drecv, lsem, fsend, frecv, hsend, hrecv, ssend, srecv):
+           pre_u, push, qdir, zdir, res, dirn, along, img, dsend, drecv, lsem, fsend, frecv, hsend, hrecv, ssend, srecv, known,
+           acc, tsend, trecv, tsems):
     case = lax.axis_index("case")
     gx = lax.axis_index("gx")
     gy = lax.axis_index("gy")
@@ -113,8 +114,22 @@
     ext[...] = jnp.zeros_like(ext)
     rem[...] = jnp.zeros_like(rem)
     rlm[...] = jnp.zeros_like(rlm)
-    for peer in peers:
+    trecv[...] = jnp.zeros_like(trecv)
+    def ring(dx, dy):
+        return device(lax.rem(gx + dx + GXN, GXN), lax.rem(gy + dy + GYN, GYN))
+
+    greeted = [ring(1, 0), ring(-1, 0), ring(0, 1), ring(0, -1)]
+    rounds = [greeted, [ring(2, 0), ring(-2, 0), ring(0, 2)], [ring(d, 0) for d in range(1, GXN)]]
+    for peer in greeted:
         pl.semaphore_signal(barrier, inc=1, device_id=peer, device_id_type=pl.DeviceIdType.MESH)
+
+    def tell(i):
+        for peer in rounds[i]:
+            pl.semaphore_signal(known.at[i], inc=1, device_id=peer, device_id_type=pl.DeviceIdType.MESH)
+
+    def hear(i):
+        pl.semaphore_wait(known.at[i], len(rounds[i]))
+
     copies = [
         pltpu.make_async_copy(factors, fac, lsem.at[0]),
         pltpu.make_async_copy(links_in, links, lsem.at[1]),
@@ -128,7 +143,7 @@
         for j in range(N):
             lm[d * N + j : d * N + j + 1, :] = jnp.full((1, B), links[d, 0, j], jnp.int32).astype(f32) * (1.0 / B)
     copies[0].wait()
-    pl.semaphore_wait(barrier, PLANE - 1)
+    pl.semaphore_wait(barrier, len(greeted))
 
     def remote(src, dst, ss, rs, sx, sy):
         return pltpu.make_async_remote_copy(
@@ -148,12 +163,15 @@
             parts.append((fac.at[pl.ds(src, count)], rem.at[pl.ds(dst, count)], n * 4 + i))
         return [remote(src, dst, fsend.at[i], frecv.at[i], sx, sy) for src, dst, i in parts[low:high]]
 
-    for sx, sy, blocks, n in moves:
+    def depart(n, low, high):
+        sx, sy, _, _ = moves[n]
         @pl.when(exists(sx, sy))
         def _():
-            for copy in rim_copies(sx, sy, blocks, n):
+            for copy in rim_copies(*moves[n], low, high):
                 copy.start()
 
+    depart(2, 0, 2)
+    tell(0)
     copies[2].wait()
 
     def square(block):
@@ -169,32 +187,31 @@
     lane_id = lax.broadcasted_iota(jnp.int32, (B, B), 1)
     eye = row_id == lane_id
 
-    def diag_at(j):
-        return pl.ds(pl.multiple_of(j * ST, 8), B)
-
     for m in range(N):
         mats[m * ST : m * ST + B, :] = jnp.where(eye, shift[m], 0.0)
     for m in range(N, 8):
         mats[m * ST : m * ST + B, :] = jnp.where(eye, 1.0, 0.0)
 
-    def own(j, carry):
-        total = mats[diag_at(j), :]
-        for d in range(4):
-            s = square(fac[d * N + j]) * lm[pl.ds(d * N + j, 1), :]
-            s = place(j, d, s)
-            total = total + s
-            if d == 1:
-                after = lax.rem(j + 1, N)
-                place(after, 5, s)
-                keep = jnp.where(j < N - 1, 1.0, 0.0)
-                mats[diag_at(after), :] = mats[diag_at(after), :] + s * keep
-        mats[diag_at(j), :] = total
-        return carry
-
-    lax.fori_loop(0, N, own, 0)
+    def ahead(n):
+        return remote(tsend.at[n], trecv.at[n], tsems.at[0, n], tsems.at[1, n], 1, 0)
+
+    half = B // 2
+    low_lanes = lax.broadcasted_iota(jnp.int32, (half // 2, B), 1) < half
+
+    def own(j):
+        s = [place(j, d, square(fac[d * N + j]) * lm[d * N + j : d * N + j + 1, :]) for d in range(4)]
+        if j < N - 1:
+            place(j + 1, 5, s[1])
+        return s
+
+    def send_ahead(n, t):
+        tsend[n, 0:half, :] = t[0:half]
+        tsend[n, half : half + half // 2, :] = jnp.where(
+            low_lanes, pltpu.roll(t[half : half + half // 2], half, 1), t[half + half // 2 :])
+        pl.when(exists(1, 0))(ahead(n).start)
 
     def arrived(n, low, high):
-        sx, sy, blocks, _ = moves[n]
+        sx, sy, _, _ = moves[n]
         @pl.when(exists(-sx, -sy))
         def _():
             for copy in rim_copies(*moves[n], low, high):
@@ -207,20 +224,46 @@
         for j, s in terms:
             mats[j * ST : j * ST + B, :] = mats[j * ST : j * ST + B, :] + s
 
+    prev = None
+    for j in range(N):
+        s = own(j)
+        mats[j * ST : j * ST + B, :] = mats[j * ST : j * ST + B, :] + ((s[0] + s[1]) + (s[2] + s[3]))
+        if j < N - 1:
+            mats[(j + 1) * ST : (j + 1) * ST + B, :] = mats[(j + 1) * ST : (j + 1) * ST + B, :] + s[1]
+        if j > 0:
+            send_ahead(j - 1, acc[j - 1] + s[3])
+        acc[j] = s[0] if prev is None else s[0] + prev
+        prev = s[2]
+        if j == 1:
+            hear(0)
+            depart(0, 0, 2)
+            depart(1, 0, 2)
+            tell(1)
+    send_ahead(N - 1, acc[N - 1])
+    depart(3, 0, 4)
+    hear(1)
+    tell(2)
+
+    arrived(2, 0, 2)
     arrived(0, 0, 2)
     arrived(1, 0, 2)
-    arrived(2, 0, 2)
     collect([
         term(0, 6, N, rlm[1, 3 * N - 1 : 3 * N, :]),
         term(N - 1, 7, 3 * N - 1, rlm[2, 3 * N : 3 * N + 1, :]),
         term(0, 5, 3 * N, rlm[3, 2 * N - 1 : 2 * N, :]),
     ])
-    arrived(3, 0, 2)
-    collect([term(j, 4, j, rlm[0, j : j + 1, :]) for j in range(N)])
-    arrived(3, 2, 3)
-    collect([term(j, 6, N + j, rlm[0, 2 * N + j - 1 : 2 * N + j, :]) for j in range(1, N)])
-    arrived(3, 3, 4)
-    collect([term(j, 7, 2 * N + j, rlm[0, 3 * N + j + 1 : 3 * N + j + 2, :]) for j in range(N - 1)])
+
+    for n in range(N):
+        pl.when(exists(-1, 0))(ahead(n).wait_recv)
+    for n in range(N):
+        top, packed = trecv[n, 0:half, :], trecv[n, half : half + half // 2, :]
+        turned = jnp.concatenate([top, jnp.zeros_like(top)], axis=0).T
+        base = n * ST
+        mats[base : base + half, :] = mats[base : base + half, :] + top
+        for k, part in enumerate((pltpu.roll(packed, half, 1), packed)):
+            at = half + k * half // 2
+            span = slice(base + at, base + at + half // 2)
+            mats[span, :] = mats[span, :] + jnp.where(low_lanes, turned[at : at + half // 2], part)
 
     for m in range(N):
         a, b, c = split3(mats[m * ST : m * ST + B, :])
@@ -229,6 +272,7 @@
         dpan[m, B : 2 * B, 0:B] = c
         dpan[m, B : 2 * B, B : 2 * B] = jnp.zeros((B, B), bf16)
     invert(mats, rpan)
+    hear(2)
 
     def pairs(terms):
         return jnp.concatenate([jnp.concatenate([t, t], axis=1) for t in terms], axis=0)
@@ -252,12 +296,6 @@
         pre[m, B : 2 * B, 0:B] = c
         pre[m, B : 2 * B, B : 2 * B] = jnp.zeros((B, B), bf16)
 
-    for sx, sy, blocks, n in moves:
-        @pl.when(exists(sx, sy))
-        def _():
-            for copy in rim_copies(sx, sy, blocks, n):
-                copy.wait_send()
-
     copies[3].wait()
     x_out[...] = jnp.zeros_like(x_out)
     dirn[...] = jnp.zeros_like(dirn)
@@ -339,6 +377,15 @@
     for j in range(N):
         ext[1, 1, 1 + j] = precondition(res[0, j], j)
     halo_start(1)
+    arrived(3, 0, 2)
+    for j in range(N):
+        term(j, 4, j, rlm[0, j : j + 1, :])
+    arrived(3, 2, 3)
+    for j in range(1, N):
+        term(j, 6, N + j, rlm[0, 2 * N + j - 1 : 2 * N + j, :])
+    arrived(3, 3, 4)
+    for j in range(N - 1):
+        term(j, 7, 2 * N + j, rlm[0, 3 * N + j + 1 : 3 * N + j + 2, :])
     halo_wait(1)
     triples = []
     for j in range(N):
@@ -347,6 +394,13 @@
         triples.append((res[0, j], u, w))
     products(0, triples)
     halo_sent(1)
+    for sx, sy, blocks, n in moves:
+        @pl.when(exists(sx, sy))
+        def _():
+            for copy in rim_copies(sx, sy, blocks, n):
+                copy.wait_send()
+    for n in range(N):
+        pl.when(exists(1, 0))(ahead(n).wait_send)
 
     def iterate(it, carry):
         gamma_old, alpha_old = carry
@@ -423,6 +477,11 @@
             pltpu.SemaphoreType.DMA((2, 8)),
             pltpu.SemaphoreType.DMA,
             pltpu.SemaphoreType.DMA((2,)),
+            pltpu.SemaphoreType.REGULAR((3,)),
+            pltpu.VMEM((N, B, B), f32),
+            pltpu.VMEM((N, 3 * B // 4, B), f32),
+            pltpu.VMEM((N, 3 * B // 4, B), f32),
+            pltpu.SemaphoreType.DMA((2, N)),
         ],
         compiler_params=pltpu.CompilerParams(collective_id=0, has_side_effects=True, vmem_limit_bytes=24 * 1024 * 1024),
         name="solve",

time: 70.6 us -> 67 us (0.949)
  Pallas kernels: 68.5 us -> 65 us
    pallas_call x1, Pallas kernels: 68.5 us -> 65 us  [local(): pl.pallas_call(kernel, out_shape=(field, field), in_specs=[hbm] * 4, out_...]
where the time goes in v5:
time: 67 us; the launch traced here: 66.9 us
  Pallas kernels  65 us (97%)
  local copies, waits for them, and re-layouts  1.28 us (2%)
    pallas_call x1, Pallas kernels, local(): pl.pallas_call(kernel, out_shape=(field, field), in_specs=[hbm] * 4, out_...  65 us

profile of v5, /device:TPU:1, one launch (start us, length us, event | category | flops | bytes accessed | tf_op | source)
XLA Modules:
  0.0 66.9 jit_solution(1948134134995261779)
XLA Ops:
  0.6 65.0 %solve.1 = (f32[1,6,32,128]{3,2,1,0:T(8,128)S(1)}, f32[1,6,32,128]{3,2,1,0:T(8,128)S(1)}) custom-call(s32[4,1,6]{2,1,0:T(1,128)} %links_in.1, f32[1,6,32,128]{3,2,1,0:T(8,128)} %load.1, bf16[24,128,128]{2,1,0:T(8,128)(2,1)} %bitcast.2, f32[6,1,128]{2,1,0:T(1,128)} %bitcast.3), custom_call_target="tpu_custom_call" | custom-call | tf_op jit(solution)/shard_map/solve/pallas_call | solution.py:445
  65.6 0.6 copy.8
  66.3 0.6 copy.9

commit v6 on v5

--- a/solution.py
+++ b/solution.py
@@ -35,21 +35,23 @@
     return a, (x - a.astype(f32)).astype(bf16)
 
 
-def invert(mats, rpan):
+def invert(mats, rpan, cpan):
     lane = lax.broadcasted_iota(jnp.int32, (8, B), 1)
-    def step(b, carry):
-        base = b * NB
-        rows = [mats[pl.ds(base + i, 8, stride=ST), :] for i in range(NB)]
-        inside = (lane >= base) & (lane < base + NB)
-        sign = jnp.where(lane < base, -1.0, jnp.where(inside, 0.0, 1.0))
-        cols = []
-        for m in range(N):
-            c0, c1, c2 = split3(mats[pl.ds(pl.multiple_of(m * ST + base, 8), 8), :] * sign)
-            cols.append(jnp.concatenate([c0, c0, c1, c1, c0, c2], axis=0))
+
+    def packed(base):
+        return [mats[pl.ds(base + i, 8, stride=ST), :] for i in range(NB)]
+
+    def pick(row, k):
+        return jnp.sum(jnp.where(lane == k, row, 0.0), axis=1, keepdims=True)
+
+    def pivot(rows, base):
         e = {}
         for j in range(NB):
             for i in range(j + 1):
-                e[i, j] = jnp.sum(jnp.where(lane == base + j, rows[i], 0.0), axis=1, keepdims=True)
+                e[i, j] = pick(rows[i], base + j)
+        ahead = [[pick(rows[k], base + NB + i) for k in range(NB)] for i in range(NB)]
+        inside = (lane >= base) & (lane < base + NB)
+        sign = jnp.where(lane < base, -1.0, jnp.where(inside, 0.0, 1.0))
         at = lambda i, j: e[min(i, j), max(i, j)]
         for k in range(NB):
             p = 1.0 / e[k, k]
@@ -64,29 +66,54 @@
                     e[min(i, k), max(i, k)] = scaled[i]
             e[k, k] = -p
         panel = [jnp.where(lane == base + i, 1.0, jnp.where(inside, 0.0, rows[i])) for i in range(NB)]
+        right = []
         for j in range(NB):
             total = None
             for i in range(NB):
                 term = at(i, j) * panel[i]
                 total = term if total is None else total + term
-            rpan[pl.ds(j, 8, stride=NB), :] = -total
+            right.append(-total)
+        following = packed(jnp.minimum(base + NB, B - NB))
+        after = []
+        for i in range(NB):
+            row = jnp.where(inside, 0.0, following[i])
+            for k in range(NB):
+                row = row - ahead[i][k] * right[k]
+            after.append(row)
+        for k in range(NB):
+            cpan[pl.ds(k, 8, stride=NB), :] = rows[k] * sign
+            rpan[pl.ds(k, 8, stride=NB), :] = right[k]
+        return tuple(after)
+
+    def trail(base):
+        inside = (lane >= base) & (lane < base + NB)
+        rows = [rpan[m * NB : (m + 1) * NB, :] for m in range(N)]
         ups = []
         for m in range(N):
-            r0, r1, r2 = split3(rpan[m * NB : (m + 1) * NB, :])
-            right = jnp.concatenate([r0, r1, r0, r1, r2, r0], axis=0)
-            ups.append(lax.dot_general(cols[m], right, (((0,), (0,)), ((), ())), preferred_element_type=f32))
+            c0, c1, c2 = split3(cpan[m * NB : (m + 1) * NB, :])
+            r0, r1, r2 = split3(rows[m])
+            ups.append(lax.dot_general(
+                jnp.concatenate([c0, c0, c1, c1, c0, c2], axis=0),
+                jnp.concatenate([r0, r1, r0, r1, r2, r0], axis=0),
+                (((0,), (0,)), ((), ())), preferred_element_type=f32))
         new = [jnp.where(inside[0:1, :], 0.0, mats[m * ST : m * ST + B, :]) - ups[m] for m in range(N)]
         for m in range(N):
             mats[m * ST : m * ST + B, :] = new[m]
         for m in range(N):
-            mats[pl.ds(pl.multiple_of(m * ST + base, 8), 8), :] = rpan[m * NB : (m + 1) * NB, :]
-        return carry
-    lax.fori_loop(0, B // NB, step, 0)
-
-
-def kernel(links_in, load, factors, shift_in, x_out, r_out, links, shift, fac, rem, lm, rlm, mats, rpan, dpan, wts, pre, ext,
+            mats[pl.ds(pl.multiple_of(m * ST + base, 8), 8), :] = rows[m]
+
+    def step(b, rows):
+        trail((b - 1) * NB)
+        return pivot(rows, b * NB)
+
+    rows = pivot(packed(0), 0)
+    lax.fori_loop(1, B // NB, step, rows)
+    trail(B - NB)
+
+
+def kernel(links_in, load, factors, shift_in, x_out, r_out, links, shift, fac, rem, lm, rlm, mats, rpan, cpan, dpan, errs, wts, pre, ext,
            pre_u, push, qdir, zdir, res, dirn, along, img, dsend, drecv, lsem, fsend, frecv, hsend, hrecv, ssend, srecv, known,
-           acc, tsend, trecv, tsems):
+           tsend, trecv, tsems):
     case = lax.axis_index("case")
     gx = lax.axis_index("gx")
     gy = lax.axis_index("gy")
@@ -195,20 +222,29 @@
     def ahead(n):
         return remote(tsend.at[n], trecv.at[n], tsems.at[0, n], tsems.at[1, n], 1, 0)
 
-    half = B // 2
-    low_lanes = lax.broadcasted_iota(jnp.int32, (half // 2, B), 1) < half
-
-    def own(j):
-        s = [place(j, d, square(fac[d * N + j]) * lm[d * N + j : d * N + j + 1, :]) for d in range(4)]
-        if j < N - 1:
-            place(j + 1, 5, s[1])
+    quarter = B // 4
+    lane_q = lax.broadcasted_iota(jnp.int32, (quarter, B), 1)
+    lane_h = lax.broadcasted_iota(jnp.int32, (quarter // 2, B), 1)
+    above = row_id // quarter <= lane_id // quarter
+
+    def own(j, d):
+        s = place(j, d, square(fac[d * N + j]) * lm[d * N + j : d * N + j + 1, :])
+        mats[j * ST : j * ST + B, :] = mats[j * ST : j * ST + B, :] + s
         return s
 
     def send_ahead(n, t):
-        tsend[n, 0:half, :] = t[0:half]
-        tsend[n, half : half + half // 2, :] = jnp.where(
-            low_lanes, pltpu.roll(t[half : half + half // 2], half, 1), t[half + half // 2 :])
+        q = [t[k * quarter : (k + 1) * quarter] for k in range(4)]
+        tsend[n, 0:quarter, :] = q[0]
+        tsend[n, quarter : 2 * quarter, :] = jnp.where(lane_q < quarter, pltpu.roll(q[3], quarter, 1), q[1])
+        tsend[n, 2 * quarter :, :] = jnp.where(
+            lane_h < 2 * quarter, pltpu.roll(q[2][: quarter // 2], 2 * quarter, 1), q[2][quarter // 2 :])
         pl.when(exists(1, 0))(ahead(n).start)
+
+    def unpack(n):
+        p0, p1, p2 = trecv[n, 0:quarter, :], trecv[n, quarter : 2 * quarter, :], trecv[n, 2 * quarter :, :]
+        upper = jnp.concatenate(
+            [p0, p1, pltpu.roll(p2, 2 * quarter, 1), p2, pltpu.roll(p1, 3 * quarter, 1)], axis=0)
+        return jnp.where(above, upper, upper.T)
 
     def arrived(n, low, high):
         sx, sy, _, _ = moves[n]
@@ -224,25 +260,28 @@
         for j, s in terms:
             mats[j * ST : j * ST + B, :] = mats[j * ST : j * ST + B, :] + s
 
-    prev = None
-    for j in range(N):
-        s = own(j)
-        mats[j * ST : j * ST + B, :] = mats[j * ST : j * ST + B, :] + ((s[0] + s[1]) + (s[2] + s[3]))
-        if j < N - 1:
-            mats[(j + 1) * ST : (j + 1) * ST + B, :] = mats[(j + 1) * ST : (j + 1) * ST + B, :] + s[1]
-        if j > 0:
-            send_ahead(j - 1, acc[j - 1] + s[3])
-        acc[j] = s[0] if prev is None else s[0] + prev
-        prev = s[2]
-        if j == 1:
+    for n in range(N):
+        t = own(n, 0)
+        if n > 0:
+            t = t + own(n - 1, 2)
+        if n < N - 1:
+            t = t + own(n + 1, 3)
+        send_ahead(n, t)
+        if n == 1:
             hear(0)
             depart(0, 0, 2)
             depart(1, 0, 2)
             tell(1)
-    send_ahead(N - 1, acc[N - 1])
     depart(3, 0, 4)
     hear(1)
     tell(2)
+    own(N - 1, 2)
+    own(0, 3)
+    for j in range(N):
+        t = own(j, 1)
+        if j < N - 1:
+            place(j + 1, 5, t)
+            mats[(j + 1) * ST : (j + 1) * ST + B, :] = mats[(j + 1) * ST : (j + 1) * ST + B, :] + t
 
     arrived(2, 0, 2)
     arrived(0, 0, 2)
@@ -256,22 +295,17 @@
     for n in range(N):
         pl.when(exists(-1, 0))(ahead(n).wait_recv)
     for n in range(N):
-        top, packed = trecv[n, 0:half, :], trecv[n, half : half + half // 2, :]
-        turned = jnp.concatenate([top, jnp.zeros_like(top)], axis=0).T
-        base = n * ST
-        mats[base : base + half, :] = mats[base : base + half, :] + top
-        for k, part in enumerate((pltpu.roll(packed, half, 1), packed)):
-            at = half + k * half // 2
-            span = slice(base + at, base + at + half // 2)
-            mats[span, :] = mats[span, :] + jnp.where(low_lanes, turned[at : at + half // 2], part)
+        mats[n * ST : n * ST + B, :] = mats[n * ST : n * ST + B, :] + unpack(n)
 
     for m in range(N):
         a, b, c = split3(mats[m * ST : m * ST + B, :])
         dpan[m, 0:B, 0:B] = a
         dpan[m, 0:B, B : 2 * B] = b
-        dpan[m, B : 2 * B, 0:B] = c
-        dpan[m, B : 2 * B, B : 2 * B] = jnp.zeros((B, B), bf16)
-    invert(mats, rpan)
+        dpan[m, B : 2 * B, 0:B] = b
+        dpan[m, B : 2 * B, B : 2 * B] = a
+        dpan[m, 0:B, 2 * B :] = a
+        dpan[m, B : 2 * B, 2 * B :] = c
+    invert(mats, rpan, cpan)
     hear(2)
 
     def pairs(terms):
@@ -281,14 +315,18 @@
         small = (out[2 * h :, 0:B] + out[2 * h :, B:]) + out[h : 2 * h, B:]
         return out[0:h, 0:B] + (out[h : 2 * h, 0:B] + (out[0:h, B:] + small))
 
+    for m in range(N):
+        a, b, c = split3(mats[m * ST : m * ST + B, :])
+        pre[m, 0:B, 0:B] = a
+        pre[m, 0:B, B : 2 * B] = b
+        large = jnp.dot(jnp.concatenate([a, b], axis=1), dpan[m, :, 0 : 2 * B], preferred_element_type=f32)
+        small = jnp.dot(jnp.concatenate([c, a], axis=1), dpan[m, :, 2 * B :], preferred_element_type=f32)
+        product = (small + large[:, B:]) + large[:, 0:B]
+        errs[m] = (jnp.where(eye, 1.0, 0.0) - product).astype(bf16)
     better = []
     for m in range(N):
-        inv = mats[m * ST : m * ST + B, :]
-        terms = split3(inv)
-        product = fold(jnp.dot(pairs(terms), dpan[m], preferred_element_type=f32), B)
-        error = (jnp.where(eye, 1.0, 0.0) - product).astype(bf16)
-        fix = jnp.dot(error, jnp.concatenate(terms[0:2], axis=1), preferred_element_type=f32)
-        better.append(inv + (fix[:, 0:B] + fix[:, B:]))
+        fix = jnp.dot(errs[m], pre[m, 0:B, :], preferred_element_type=f32)
+        better.append(mats[m * ST : m * ST + B, :] + (fix[:, 0:B] + fix[:, B:]))
     for m in range(N):
         a, b, c = split3(better[m])
         pre[m, 0:B, 0:B] = a
@@ -456,7 +494,9 @@
             pltpu.VMEM((4, 4 * N, B), f32),
             pltpu.VMEM((8 * ST, B), f32),
             pltpu.VMEM((8 * NB, B), f32),
-            pltpu.VMEM((N, 2 * B, 2 * B), bf16),
+            pltpu.VMEM((8 * NB, B), f32),
+            pltpu.VMEM((N, 2 * B, 3 * B), bf16),
+            pltpu.VMEM((N, B, B), bf16),
             pltpu.VMEM((N, 8 * B, 2 * B), bf16),
             pltpu.VMEM((N, 2 * B, 2 * B), bf16),
             pltpu.VMEM((2, 3, N + 2, R, B), f32),
@@ -478,9 +518,8 @@
             pltpu.SemaphoreType.DMA,
             pltpu.SemaphoreType.DMA((2,)),
             pltpu.SemaphoreType.REGULAR((3,)),
-            pltpu.VMEM((N, B, B), f32),
-            pltpu.VMEM((N, 3 * B // 4, B), f32),
-            pltpu.VMEM((N, 3 * B // 4, B), f32),
+            pltpu.VMEM((N, 5 * B // 8, B), f32),
+            pltpu.VMEM((N, 5 * B // 8, B), f32),
             pltpu.SemaphoreType.DMA((2, N)),
         ],
         compiler_params=pltpu.CompilerParams(collective_id=0, has_side_effects=True, vmem_limit_bytes=24 * 1024 * 1024),

time: 67 us -> 64.2 us (0.958)
  Pallas kernels: 65 us -> 62.1 us
    pallas_call x1, Pallas kernels: 65 us -> 62.1 us  [local(): pl.pallas_call(kernel, out_shape=(field, field), in_specs=[hbm] * 4, out_...]
where the time goes in v6:
time: 64.2 us; the launch traced here: 64.1 us
  Pallas kernels  62.1 us (97%)
  local copies, waits for them, and re-layouts  1.28 us (2%)
    pallas_call x1, Pallas kernels, local(): pl.pallas_call(kernel, out_shape=(field, field), in_specs=[hbm] * 4, out_...  62.1 us

profile of v6, /device:TPU:1, one launch (start us, length us, event | category | flops | bytes accessed | tf_op | source)
XLA Modules:
  0.0 64.1 jit_solution(10772964295197767883)
XLA Ops:
  0.6 62.1 %solve.1 = (f32[1,6,32,128]{3,2,1,0:T(8,128)S(1)}, f32[1,6,32,128]{3,2,1,0:T(8,128)S(1)}) custom-call(s32[4,1,6]{2,1,0:T(1,128)} %links_in.1, f32[1,6,32,128]{3,2,1,0:T(8,128)} %load.1, bf16[24,128,128]{2,1,0:T(8,128)(2,1)} %bitcast.2, f32[6,1,128]{2,1,0:T(1,128)} %bitcast.3), custom_call_target="tpu_custom_call" | custom-call | tf_op jit(solution)/shard_map/solve/pallas_call | solution.py:483
  62.8 0.6 %copy.8 = f32[1,6,32,128]{3,2,1,0:T(8,128)} copy(f32[1,6,32,128]{3,2,1,0:T(8,128)S(1)} %get-tuple-element.4) | data formatting | bytes 196608
  63.4 0.6 copy.9

commit v7 on v6

--- a/solution.py
+++ b/solution.py
@@ -133,15 +133,11 @@
 
     barrier = pltpu.get_barrier_semaphore()
     peers = []
-    for a in (4, 3, 5, 2, 6, 1, 7, 0):
-        for c in (2, 1, 3, 0):
-            if a or c:
-                peers.append(device(lax.rem(gx + a, GXN), lax.rem(gy + c, GYN)))
-
-    ext[...] = jnp.zeros_like(ext)
-    rem[...] = jnp.zeros_like(rem)
-    rlm[...] = jnp.zeros_like(rlm)
-    trecv[...] = jnp.zeros_like(trecv)
+    hops = lambda a, c: -(min((a + 1) // 2, (GXN - a + 1) // 2) + min(c, GYN - c))
+    for a, c in sorted([(a, c) for a in range(GXN) for c in range(GYN)], key=lambda t: hops(*t)):
+        if a or c:
+            peers.append(device(lax.rem(gx + a, GXN), lax.rem(gy + c, GYN)))
+
     def ring(dx, dy):
         return device(lax.rem(gx + dx + GXN, GXN), lax.rem(gy + dy + GYN, GYN))
 
@@ -170,7 +166,6 @@
         for j in range(N):
             lm[d * N + j : d * N + j + 1, :] = jnp.full((1, B), links[d, 0, j], jnp.int32).astype(f32) * (1.0 / B)
     copies[0].wait()
-    pl.semaphore_wait(barrier, len(greeted))
 
     def remote(src, dst, ss, rs, sx, sy):
         return pltpu.make_async_remote_copy(
@@ -197,8 +192,6 @@
             for copy in rim_copies(*moves[n], low, high):
                 copy.start()
 
-    depart(2, 0, 2)
-    tell(0)
     copies[2].wait()
 
     def square(block):
@@ -238,7 +231,6 @@
         tsend[n, quarter : 2 * quarter, :] = jnp.where(lane_q < quarter, pltpu.roll(q[3], quarter, 1), q[1])
         tsend[n, 2 * quarter :, :] = jnp.where(
             lane_h < 2 * quarter, pltpu.roll(q[2][: quarter // 2], 2 * quarter, 1), q[2][quarter // 2 :])
-        pl.when(exists(1, 0))(ahead(n).start)
 
     def unpack(n):
         p0, p1, p2 = trecv[n, 0:quarter, :], trecv[n, quarter : 2 * quarter, :], trecv[n, 2 * quarter :, :]
@@ -260,14 +252,26 @@
         for j, s in terms:
             mats[j * ST : j * ST + B, :] = mats[j * ST : j * ST + B, :] + s
 
-    for n in range(N):
+    def first(n):
         t = own(n, 0)
         if n > 0:
             t = t + own(n - 1, 2)
         if n < N - 1:
             t = t + own(n + 1, 3)
         send_ahead(n, t)
-        if n == 1:
+
+    early = 2
+    for n in range(early):
+        first(n)
+    pl.semaphore_wait(barrier, len(greeted))
+    for n in range(early):
+        pl.when(exists(1, 0))(ahead(n).start)
+    depart(2, 0, 2)
+    tell(0)
+    for n in range(early, N):
+        first(n)
+        pl.when(exists(1, 0))(ahead(n).start)
+        if n == early:
             hear(0)
             depart(0, 0, 2)
             depart(1, 0, 2)
@@ -282,6 +286,33 @@
         if j < N - 1:
             place(j + 1, 5, t)
             mats[(j + 1) * ST : (j + 1) * ST + B, :] = mats[(j + 1) * ST : (j + 1) * ST + B, :] + t
+
+    def clear(ref, *spans):
+        for span in spans:
+            ref[span] = jnp.zeros_like(ref[span])
+
+    @pl.when(gx == 0)
+    def _():
+        clear(ext, (slice(None), 0))
+        clear(rem, slice(0, 3 * N))
+        clear(rlm, slice(0, 3))
+        clear(trecv, slice(None))
+
+    @pl.when(gx == GXN - 1)
+    def _():
+        clear(ext, (slice(None), 2))
+
+    @pl.when(gy == 0)
+    def _():
+        clear(ext, (slice(None), slice(None), 0))
+        clear(rem, N, 3 * N)
+        clear(rlm, 1, 3)
+
+    @pl.when(gy == GYN - 1)
+    def _():
+        clear(ext, (slice(None), slice(None), N + 1))
+        clear(rem, 3 * N - 1)
+        clear(rlm, 2)
 
     arrived(2, 0, 2)
     arrived(0, 0, 2)
@@ -335,11 +366,6 @@
         pre[m, B : 2 * B, B : 2 * B] = jnp.zeros((B, B), bf16)
 
     copies[3].wait()
-    x_out[...] = jnp.zeros_like(x_out)
-    dirn[...] = jnp.zeros_like(dirn)
-    along[...] = jnp.zeros_like(along)
-    qdir[...] = jnp.zeros_like(qdir)
-    zdir[...] = jnp.zeros_like(zdir)
 
     def precondition(v, m):
         return fold(jnp.dot(pairs(split3(v)), pre[m], preferred_element_type=f32), R)
@@ -386,29 +412,34 @@
             send_sem=ssend, recv_sem=srecv.at[par],
             device_id=peer, device_id_type=pl.DeviceIdType.MESH)
 
+    def scatter(par, sums):
+        spread = 0.0
+        for k, t in reversed(list(enumerate(sums))):
+            spread = jnp.where(lane == rhs + k * R, jnp.sum(t, axis=1, keepdims=True), spread)
+        row = jnp.sum(spread, axis=0, keepdims=True)
+        dsend[pl.ds(par, 1), :] = row
+        drecv[par, pl.ds(me, 1), :] = row
+        for peer in peers:
+            contribution(par, peer).start()
+
+    def gather(par, count):
+        everything = drecv.at[par, pl.ds(0, PLANE - 1)]
+        pltpu.make_async_copy(everything, everything, srecv.at[par]).wait()
+        pltpu.make_async_copy(everything, everything, ssend).wait()
+        total = jnp.sum(drecv[par], axis=0, keepdims=True)
+        return [jnp.sum(jnp.where(lane == rhs + k * R, total, 0.0), axis=1, keepdims=True) for k in range(count)]
+
     def products(par, triples):
         gsum, dsum = None, None
         for r, u, w in triples:
             g, d = u * r, u * w
             gsum = g if gsum is None else gsum + g
             dsum = d if dsum is None else dsum + d
-        gcol = jnp.sum(gsum, axis=1, keepdims=True)
-        dcol = jnp.sum(dsum, axis=1, keepdims=True)
-        spread = jnp.where(lane == rhs, gcol, jnp.where(lane == rhs + R, dcol, 0.0))
-        row = jnp.sum(spread, axis=0, keepdims=True)
-        dsend[pl.ds(par, 1), :] = row
-        drecv[par, pl.ds(me, 1), :] = row
-        for peer in peers:
-            contribution(par, peer).start()
-
-    def totals(par, first, gamma_old, alpha_old):
-        everything = drecv.at[par, pl.ds(0, PLANE - 1)]
-        pltpu.make_async_copy(everything, everything, srecv.at[par]).wait()
-        pltpu.make_async_copy(everything, everything, ssend).wait()
-        total = jnp.sum(drecv[par], axis=0, keepdims=True)
-        gamma = jnp.sum(jnp.where(lane == rhs, total, 0.0), axis=1, keepdims=True)
-        delta = jnp.sum(jnp.where(lane == rhs + R, total, 0.0), axis=1, keepdims=True)
-        ratio = jnp.where(first, 0.0, gamma / gamma_old)
+        scatter(par, [gsum, dsum])
+
+    def totals(par, gamma_old, alpha_old):
+        gamma, delta = gather(par, 2)
+        ratio = gamma / gamma_old
         alpha = gamma / (delta - ratio * gamma / alpha_old)
         return gamma, ratio, alpha
 
@@ -425,11 +456,44 @@
     for j in range(N - 1):
         term(j, 7, 2 * N + j, rlm[0, 3 * N + j + 1 : 3 * N + j + 2, :])
     halo_wait(1)
+    for j in range(N):
+        pre_u[j], img[j] = ext[1, 1, 1 + j], operate(1, j)
+    halo_sent(1)
+
+    for j in range(N):
+        ext[0, 1, 1 + j] = precondition(img[j], j)
+    halo_start(0)
+    halo_wait(0)
+    groups = []
+    for j in range(N):
+        u, w, m, n = pre_u[j], img[j], ext[0, 1, 1 + j], operate(0, j)
+        push[j] = n
+        groups.append((u * res[0, j], u * w, w * m, n * m))
+    scatter(1, [sum(g[1:], g[0]) for g in zip(*groups)])
+    for j in range(N):
+        ext[1, 1, 1 + j] = precondition(push[j], j)
+    halo_sent(0)
+    halo_start(1)
+    halo_wait(1)
+    for j in range(N):
+        zdir[j] = operate(1, j)
+    gamma, delta, wm, nm = gather(1, 4)
+    alpha = gamma / delta
+    gamma_next = gamma - alpha * (2.0 * delta - alpha * wm)
+    delta_next = delta - alpha * (2.0 * wm - alpha * nm)
+    ratio = gamma_next / gamma
+    alpha_next = gamma_next / (delta_next - ratio * gamma_next / alpha)
     triples = []
     for j in range(N):
-        u, w = ext[1, 1, 1 + j], operate(1, j)
-        pre_u[j], img[j] = u, w
-        triples.append((res[0, j], u, w))
+        u, w, m, n, o, t = pre_u[j], img[j], ext[0, 1, 1 + j], push[j], ext[1, 1, 1 + j], zdir[j]
+        u1, w1, m1, n1 = u - alpha * m, w - alpha * n, m - alpha * o, n - alpha * t
+        p, s, q, z = u1 + ratio * u, w1 + ratio * w, m1 + ratio * m, n1 + ratio * n
+        zdir[j], qdir[j], along[j], dirn[j] = z, q, s, p
+        x_out[0, j] = alpha * u + alpha_next * p
+        r = res[0, j] - alpha * w - alpha_next * s
+        u2, w2 = u1 - alpha_next * q, w1 - alpha_next * z
+        res[0, j], pre_u[j], img[j] = r, u2, w2
+        triples.append((r, u2, w2))
     products(0, triples)
     halo_sent(1)
     for sx, sy, blocks, n in moves:
@@ -449,7 +513,7 @@
         halo_wait(par)
         for j in range(N):
             push[j] = operate(par, j)
-        gamma, ratio, alpha = totals(par, it == 0, gamma_old, alpha_old)
+        gamma, ratio, alpha = totals(par, gamma_old, alpha_old)
         triples = []
         for j in range(N):
             u, w = pre_u[j], img[j]
@@ -468,9 +532,8 @@
         halo_sent(par)
         return gamma, alpha
 
-    one = jnp.ones((R, 1), f32)
-    gamma_old, alpha_old = lax.fori_loop(0, ITERS - 1, iterate, (one, one))
-    gamma, ratio, alpha = totals((ITERS - 1) % 2, ITERS == 1, gamma_old, alpha_old)
+    gamma_old, alpha_old = lax.fori_loop(2, ITERS - 1, iterate, (gamma_next, alpha_next))
+    gamma, ratio, alpha = totals((ITERS - 1) % 2, gamma_old, alpha_old)
     for j in range(N):
         x_out[0, j] = x_out[0, j] + alpha * (pre_u[j] + ratio * dirn[j])
         r_out[0, j] = res[0, j] - alpha * (img[j] + ratio * along[j])

time: 64.2 us -> 63.3 us (0.986)
  Pallas kernels: 62.1 us -> 61.3 us
    pallas_call x1, Pallas kernels: 62.1 us -> 61.3 us  [local(): pl.pallas_call(kernel, out_shape=(field, field), in_specs=[hbm] * 4, out_...]
where the time goes in v7:
time: 63.3 us; the launch traced here: 63.2 us
  Pallas kernels  61.3 us (97%)
  local copies, waits for them, and re-layouts  1.28 us (2%)
  between operations  0.64 us (1%)
    pallas_call x1, Pallas kernels, local(): pl.pallas_call(kernel, out_shape=(field, field), in_specs=[hbm] * 4, out_...  61.3 us
    unnamed x2, local copies, waits for them, and re-layouts  1.28 us

profile of v7, /device:TPU:1, one launch (start us, length us, event | category | flops | bytes accessed | tf_op | source)
XLA Modules:
  0.0 63.2 jit_solution(5508821693215215357)
XLA Ops:
  0.6 61.3 %solve.1 = (f32[1,6,32,128]{3,2,1,0:T(8,128)S(1)}, f32[1,6,32,128]{3,2,1,0:T(8,128)S(1)}) custom-call(s32[4,1,6]{2,1,0:T(1,128)} %links_in.1, f32[1,6,32,128]{3,2,1,0:T(8,128)} %load.1, bf16[24,128,128]{2,1,0:T(8,128)(2,1)} %bitcast.2, f32[6,1,128]{2,1,0:T(1,128)} %bitcast.3), custom_call_target="tpu_custom_call" | custom-call | tf_op jit(solution)/shard_map/solve/pallas_call | solution.py:546
  61.9 0.6 %copy.8 = f32[1,6,32,128]{3,2,1,0:T(8,128)} copy(f32[1,6,32,128]{3,2,1,0:T(8,128)S(1)} %get-tuple-element.4) | data formatting | bytes 196608
  62.6 0.6 %copy.9 = f32[1,6,32,128]{3,2,1,0:T(8,128)} copy(f32[1,6,32,128]{3,2,1,0:T(8,128)S(1)} %get-tuple-element.5) | data formatting | bytes 196608

commit v8 on v7

--- a/solution.py
+++ b/solution.py
@@ -16,6 +16,7 @@
 GXN = 8
 GYN = 4
 PLANE = GXN * GYN
+CUT = 3
 OFFSETS = ((1, 0), (0, 1), (1, 1), (1, -1))
 SIDES = ((1, 1), (1, -1), (-1, 1), (-1, -1), (1, 0), (-1, 0), (0, 1), (0, -1))
 f32 = jnp.float32
@@ -381,27 +382,39 @@
         out = fold(jnp.dot(left, wts[j], preferred_element_type=f32), R)
         return out + shift[j] * centre
 
-    def halo(par):
-        for n, (sx, sy) in enumerate(SIDES):
+    def halo(par, part=None):
+        n = 0
+        for sx, sy in SIDES:
             if sy == 0:
-                src = ext.at[par, 1, pl.ds(1, N)]
-                dst = ext.at[par, 1 - sx, pl.ds(1, N)]
+                pieces = [(pl.ds(1 + low, high - low), pl.ds(1 + low, high - low)) for low, high in ((0, CUT), (CUT, N))]
             else:
-                src = ext.at[par, 1, N if sy == 1 else 1]
-                dst = ext.at[par, 1 - sx, 0 if sy == 1 else N + 1]
-            yield sx, sy, remote(src, dst, hsend.at[n], hrecv.at[par, n], sx, sy)
+                pieces = [(N if sy == 1 else 1, 0 if sy == 1 else N + 1)]
+            for k, (src, dst) in enumerate(pieces):
+                if part is None or part == k:
+                    yield sx, sy, remote(ext.at[par, 1, src], ext.at[par, 1 - sx, dst],
+                                         hsend.at[n], hrecv.at[par, n], sx, sy)
+                n += 1
 
     def halo_start(par):
-        for sx, sy, copy in halo(par):
-            pl.when(exists(sx, sy))(copy.start)
-
-    def halo_wait(par):
-        for sx, sy, copy in halo(par):
+        for part in range(2):
+            for sx, sy, copy in halo(par, part):
+                pl.when(exists(sx, sy))(copy.start)
+
+    def halo_wait(par, part):
+        for sx, sy, copy in halo(par, part):
             pl.when(exists(-sx, -sy))(copy.wait_recv)
 
     def halo_sent(par):
         for sx, sy, copy in halo(par):
             pl.when(exists(sx, sy))(copy.wait_send)
+
+    def apply(par, out):
+        halo_wait(par, 0)
+        for j in range(CUT - 1):
+            out[j] = operate(par, j)
+        halo_wait(par, 1)
+        for j in range(CUT - 1, N):
+            out[j] = operate(par, j)
 
     lane = lax.broadcasted_iota(jnp.int32, (R, B), 1)
     rhs = lax.broadcasted_iota(jnp.int32, (R, B), 0)
@@ -455,28 +468,25 @@
     arrived(3, 3, 4)
     for j in range(N - 1):
         term(j, 7, 2 * N + j, rlm[0, 3 * N + j + 1 : 3 * N + j + 2, :])
-    halo_wait(1)
-    for j in range(N):
-        pre_u[j], img[j] = ext[1, 1, 1 + j], operate(1, j)
+    apply(1, img)
+    for j in range(N):
+        pre_u[j] = ext[1, 1, 1 + j]
     halo_sent(1)
 
     for j in range(N):
         ext[0, 1, 1 + j] = precondition(img[j], j)
     halo_start(0)
-    halo_wait(0)
+    apply(0, push)
     groups = []
     for j in range(N):
-        u, w, m, n = pre_u[j], img[j], ext[0, 1, 1 + j], operate(0, j)
-        push[j] = n
+        u, w, m, n = pre_u[j], img[j], ext[0, 1, 1 + j], push[j]
         groups.append((u * res[0, j], u * w, w * m, n * m))
     scatter(1, [sum(g[1:], g[0]) for g in zip(*groups)])
     for j in range(N):
         ext[1, 1, 1 + j] = precondition(push[j], j)
     halo_sent(0)
     halo_start(1)
-    halo_wait(1)
-    for j in range(N):
-        zdir[j] = operate(1, j)
+    apply(1, zdir)
     gamma, delta, wm, nm = gather(1, 4)
     alpha = gamma / delta
     gamma_next = gamma - alpha * (2.0 * delta - alpha * wm)
@@ -510,9 +520,7 @@
         for j in range(N):
             ext[par, 1, 1 + j] = precondition(img[j], j)
         halo_start(par)
-        halo_wait(par)
-        for j in range(N):
-            push[j] = operate(par, j)
+        apply(par, push)
         gamma, ratio, alpha = totals(par, gamma_old, alpha_old)
         triples = []
         for j in range(N):
@@ -576,8 +584,8 @@
             pltpu.SemaphoreType.DMA((4,)),
             pltpu.SemaphoreType.DMA((16,)),
             pltpu.SemaphoreType.DMA((16,)),
-            pltpu.SemaphoreType.DMA((8,)),
-            pltpu.SemaphoreType.DMA((2, 8)),
+            pltpu.SemaphoreType.DMA((10,)),
+            pltpu.SemaphoreType.DMA((2, 10)),
             pltpu.SemaphoreType.DMA,
             pltpu.SemaphoreType.DMA((2,)),
             pltpu.SemaphoreType.REGULAR((3,)),

time: 63.3 us -> 62.8 us (level)
  no operation moved by 1% of the time
where the time goes in v8:
time: 62.8 us; the launch traced here: 62.7 us
  Pallas kernels  60.7 us (97%)
  local copies, waits for them, and re-layouts  1.28 us (2%)
  between operations  0.64 us (1%)
    pallas_call x1, Pallas kernels, local(): pl.pallas_call(kernel, out_shape=(field, field), in_specs=[hbm] * 4, out_...  60.7 us
    unnamed x2, local copies, waits for them, and re-layouts  1.28 us

profile of v8, /device:TPU:1, one launch (start us, length us, event | category | flops | bytes accessed | tf_op | source)
XLA Modules:
  0.0 62.7 jit_solution(2393780347966680976)
XLA Ops:
  0.6 60.7 %solve.1 = (f32[1,6,32,128]{3,2,1,0:T(8,128)S(1)}, f32[1,6,32,128]{3,2,1,0:T(8,128)S(1)}) custom-call(s32[4,1,6]{2,1,0:T(1,128)} %links_in.1, f32[1,6,32,128]{3,2,1,0:T(8,128)} %load.1, bf16[24,128,128]{2,1,0:T(8,128)(2,1)} %bitcast.2, f32[6,1,128]{2,1,0:T(1,128)} %bitcast.3), custom_call_target="tpu_custom_call" | custom-call | tf_op jit(solution)/shard_map/solve/pallas_call | solution.py:554
  61.4 0.6 %copy.8 = f32[1,6,32,128]{3,2,1,0:T(8,128)} copy(f32[1,6,32,128]{3,2,1,0:T(8,128)S(1)} %get-tuple-element.4) | data formatting | bytes 196608
  62.0 0.6 %copy.9 = f32[1,6,32,128]{3,2,1,0:T(8,128)} copy(f32[1,6,32,128]{3,2,1,0:T(8,128)S(1)} %get-tuple-element.5) | data formatting | bytes 196608

commit v9 on v8

--- a/solution.py
+++ b/solution.py
@@ -366,6 +366,8 @@
         pre[m, B : 2 * B, 0:B] = c
         pre[m, B : 2 * B, B : 2 * B] = jnp.zeros((B, B), bf16)
 
+    for ref in (x_out, dirn, along, qdir, zdir):
+        ref[...] = jnp.zeros_like(ref)
     copies[3].wait()
 
     def precondition(v, m):
@@ -450,9 +452,9 @@
             dsum = d if dsum is None else dsum + d
         scatter(par, [gsum, dsum])
 
-    def totals(par, gamma_old, alpha_old):
+    def totals(par, first, gamma_old, alpha_old):
         gamma, delta = gather(par, 2)
-        ratio = gamma / gamma_old
+        ratio = jnp.where(first, 0.0, gamma / gamma_old)
         alpha = gamma / (delta - ratio * gamma / alpha_old)
         return gamma, ratio, alpha
 
@@ -473,39 +475,7 @@
         pre_u[j] = ext[1, 1, 1 + j]
     halo_sent(1)
 
-    for j in range(N):
-        ext[0, 1, 1 + j] = precondition(img[j], j)
-    halo_start(0)
-    apply(0, push)
-    groups = []
-    for j in range(N):
-        u, w, m, n = pre_u[j], img[j], ext[0, 1, 1 + j], push[j]
-        groups.append((u * res[0, j], u * w, w * m, n * m))
-    scatter(1, [sum(g[1:], g[0]) for g in zip(*groups)])
-    for j in range(N):
-        ext[1, 1, 1 + j] = precondition(push[j], j)
-    halo_sent(0)
-    halo_start(1)
-    apply(1, zdir)
-    gamma, delta, wm, nm = gather(1, 4)
-    alpha = gamma / delta
-    gamma_next = gamma - alpha * (2.0 * delta - alpha * wm)
-    delta_next = delta - alpha * (2.0 * wm - alpha * nm)
-    ratio = gamma_next / gamma
-    alpha_next = gamma_next / (delta_next - ratio * gamma_next / alpha)
-    triples = []
-    for j in range(N):
-        u, w, m, n, o, t = pre_u[j], img[j], ext[0, 1, 1 + j], push[j], ext[1, 1, 1 + j], zdir[j]
-        u1, w1, m1, n1 = u - alpha * m, w - alpha * n, m - alpha * o, n - alpha * t
-        p, s, q, z = u1 + ratio * u, w1 + ratio * w, m1 + ratio * m, n1 + ratio * n
-        zdir[j], qdir[j], along[j], dirn[j] = z, q, s, p
-        x_out[0, j] = alpha * u + alpha_next * p
-        r = res[0, j] - alpha * w - alpha_next * s
-        u2, w2 = u1 - alpha_next * q, w1 - alpha_next * z
-        res[0, j], pre_u[j], img[j] = r, u2, w2
-        triples.append((r, u2, w2))
-    products(0, triples)
-    halo_sent(1)
+    products(0, [(res[0, j], pre_u[j], img[j]) for j in range(N)])
     for sx, sy, blocks, n in moves:
         @pl.when(exists(sx, sy))
         def _():
@@ -521,7 +491,7 @@
             ext[par, 1, 1 + j] = precondition(img[j], j)
         halo_start(par)
         apply(par, push)
-        gamma, ratio, alpha = totals(par, gamma_old, alpha_old)
+        gamma, ratio, alpha = totals(par, it == 0, gamma_old, alpha_old)
         triples = []
         for j in range(N):
             u, w = pre_u[j], img[j]
@@ -540,8 +510,9 @@
         halo_sent(par)
         return gamma, alpha
 
-    gamma_old, alpha_old = lax.fori_loop(2, ITERS - 1, iterate, (gamma_next, alpha_next))
-    gamma, ratio, alpha = totals((ITERS - 1) % 2, gamma_old, alpha_old)
+    one = jnp.ones((R, 1), f32)
+    gamma_old, alpha_old = lax.fori_loop(0, ITERS - 1, iterate, (one, one))
+    gamma, ratio, alpha = totals((ITERS - 1) % 2, ITERS == 1, gamma_old, alpha_old)
     for j in range(N):
         x_out[0, j] = x_out[0, j] + alpha * (pre_u[j] + ratio * dirn[j])
         r_out[0, j] = res[0, j] - alpha * (img[j] + ratio * along[j])

time: 62.8 us -> 63.3 us (level)
  no operation moved by 1% of the time
where the time goes in v9:
time: 63.3 us; the launch traced here: 63.2 us
  Pallas kernels  61.3 us (97%)
  local copies, waits for them, and re-layouts  1.28 us (2%)
  between operations  0.64 us (1%)
    pallas_call x1, Pallas kernels, local(): pl.pallas_call(kernel, out_shape=(field, field), in_specs=[hbm] * 4, out_...  61.3 us
    unnamed x2, local copies, waits for them, and re-layouts  1.28 us

profile of v9, /device:TPU:1, one launch (start us, length us, event | category | flops | bytes accessed | tf_op | source)
XLA Modules:
  0.0 63.2 jit_solution(4242976119420524812)
XLA Ops:
  0.6 61.3 %solve.1 = (f32[1,6,32,128]{3,2,1,0:T(8,128)S(1)}, f32[1,6,32,128]{3,2,1,0:T(8,128)S(1)}) custom-call(s32[4,1,6]{2,1,0:T(1,128)} %links_in.1, f32[1,6,32,128]{3,2,1,0:T(8,128)} %load.1, bf16[24,128,128]{2,1,0:T(8,128)(2,1)} %bitcast.2, f32[6,1,128]{2,1,0:T(1,128)} %bitcast.3), custom_call_target="tpu_custom_call" | custom-call | tf_op jit(solution)/shard_map/solve/pallas_call | solution.py:525
  61.9 0.6 %copy.8 = f32[1,6,32,128]{3,2,1,0:T(8,128)} copy(f32[1,6,32,128]{3,2,1,0:T(8,128)S(1)} %get-tuple-element.4) | data formatting | bytes 196608
  62.6 0.6 %copy.9 = f32[1,6,32,128]{3,2,1,0:T(8,128)} copy(f32[1,6,32,128]{3,2,1,0:T(8,128)S(1)} %get-tuple-element.5) | data formatting | bytes 196608

commit v10 on v9

--- a/solution.py
+++ b/solution.py
@@ -36,7 +36,7 @@
     return a, (x - a.astype(f32)).astype(bf16)
 
 
-def invert(mats, rpan, cpan):
+def invert(mats, rpan, cpan, turned):
     lane = lax.broadcasted_iota(jnp.int32, (8, B), 1)
 
     def packed(base):
@@ -53,6 +53,11 @@
         ahead = [[pick(rows[k], base + NB + i) for k in range(NB)] for i in range(NB)]
         inside = (lane >= base) & (lane < base + NB)
         sign = jnp.where(lane < base, -1.0, jnp.where(inside, 0.0, 1.0))
+        for k in range(NB):
+            cpan[pl.ds(k, 8, stride=NB), :] = rows[k] * sign
+        for m in range(N):
+            c0, c1, c2 = split3(cpan[m * NB : (m + 1) * NB, :])
+            turned[m] = jnp.concatenate([c0, c0, c1, c1, c0, c2], axis=0).T
         at = lambda i, j: e[min(i, j), max(i, j)]
         for k in range(NB):
             p = 1.0 / e[k, k]
@@ -82,7 +87,6 @@
                 row = row - ahead[i][k] * right[k]
             after.append(row)
         for k in range(NB):
-            cpan[pl.ds(k, 8, stride=NB), :] = rows[k] * sign
             rpan[pl.ds(k, 8, stride=NB), :] = right[k]
         return tuple(after)
 
@@ -91,12 +95,9 @@
         rows = [rpan[m * NB : (m + 1) * NB, :] for m in range(N)]
         ups = []
         for m in range(N):
-            c0, c1, c2 = split3(cpan[m * NB : (m + 1) * NB, :])
             r0, r1, r2 = split3(rows[m])
-            ups.append(lax.dot_general(
-                jnp.concatenate([c0, c0, c1, c1, c0, c2], axis=0),
-                jnp.concatenate([r0, r1, r0, r1, r2, r0], axis=0),
-                (((0,), (0,)), ((), ())), preferred_element_type=f32))
+            ups.append(jnp.dot(turned[m], jnp.concatenate([r0, r1, r0, r1, r2, r0], axis=0),
+                               preferred_element_type=f32))
         new = [jnp.where(inside[0:1, :], 0.0, mats[m * ST : m * ST + B, :]) - ups[m] for m in range(N)]
         for m in range(N):
             mats[m * ST : m * ST + B, :] = new[m]
@@ -112,7 +113,7 @@
     trail(B - NB)
 
 
-def kernel(links_in, load, factors, shift_in, x_out, r_out, links, shift, fac, rem, lm, rlm, mats, rpan, cpan, dpan, errs, wts, pre, ext,
+def kernel(links_in, load, factors, shift_in, x_out, r_out, links, shift, fac, rem, lm, rlm, mats, rpan, cpan, turned, dpan, errs, wts, pre, ext,
            pre_u, push, qdir, zdir, res, dirn, along, img, dsend, drecv, lsem, fsend, frecv, hsend, hrecv, ssend, srecv, known,
            tsend, trecv, tsems):
     case = lax.axis_index("case")
@@ -337,7 +338,7 @@
         dpan[m, B : 2 * B, B : 2 * B] = a
         dpan[m, 0:B, 2 * B :] = a
         dpan[m, B : 2 * B, 2 * B :] = c
-    invert(mats, rpan, cpan)
+    invert(mats, rpan, cpan, turned)
     hear(2)
 
     def pairs(terms):
@@ -500,13 +501,14 @@
             s = w + ratio * along[j]
             p = u + ratio * dirn[j]
             zdir[j], qdir[j], along[j], dirn[j] = z, q, s, p
-            x_out[0, j] = x_out[0, j] + alpha * p
             r = res[0, j] - alpha * s
             u = u - alpha * q
             w = w - alpha * z
             res[0, j], pre_u[j], img[j] = r, u, w
             triples.append((r, u, w))
         products(1 - par, triples)
+        for j in range(N):
+            x_out[0, j] = x_out[0, j] + alpha * dirn[j]
         halo_sent(par)
         return gamma, alpha
 
@@ -537,6 +539,7 @@
             pltpu.VMEM((8 * ST, B), f32),
             pltpu.VMEM((8 * NB, B), f32),
             pltpu.VMEM((8 * NB, B), f32),
+            pltpu.VMEM((N, B, 6 * NB), bf16),
             pltpu.VMEM((N, 2 * B, 3 * B), bf16),
             pltpu.VMEM((N, B, B), bf16),
             pltpu.VMEM((N, 8 * B, 2 * B), bf16),

time: 63.3 us -> 63 us (level)
  no operation moved by 1% of the time
where the time goes in v10:
time: 63 us; the launch traced here: 62.9 us
  Pallas kernels  61 us (97%)
  local copies, waits for them, and re-layouts  1.28 us (2%)
  between operations  0.64 us (1%)
    pallas_call x1, Pallas kernels, local(): pl.pallas_call(kernel, out_shape=(field, field), in_specs=[hbm] * 4, out_...  61 us
    unnamed x2, local copies, waits for them, and re-layouts  1.28 us

profile of v10, /device:TPU:1, one launch (start us, length us, event | category | flops | bytes accessed | tf_op | source)
XLA Modules:
  0.0 62.9 jit_solution(11998905796573652339)
XLA Ops:
  0.6 61.0 %solve.1 = (f32[1,6,32,128]{3,2,1,0:T(8,128)S(1)}, f32[1,6,32,128]{3,2,1,0:T(8,128)S(1)}) custom-call(s32[4,1,6]{2,1,0:T(1,128)} %links_in.1, f32[1,6,32,128]{3,2,1,0:T(8,128)} %load.1, bf16[24,128,128]{2,1,0:T(8,128)(2,1)} %bitcast.2, f32[6,1,128]{2,1,0:T(1,128)} %bitcast.3), custom_call_target="tpu_custom_call" | custom-call | tf_op jit(solution)/shard_map/solve/pallas_call | solution.py:527
  61.6 0.6 %copy.8 = f32[1,6,32,128]{3,2,1,0:T(8,128)} copy(f32[1,6,32,128]{3,2,1,0:T(8,128)S(1)} %get-tuple-element.4) | data formatting | bytes 196608
  62.3 0.6 %copy.9 = f32[1,6,32,128]{3,2,1,0:T(8,128)} copy(f32[1,6,32,128]{3,2,1,0:T(8,128)S(1)} %get-tuple-element.5) | data formatting | bytes 196608

commit v11 on v10

--- a/solution.py
+++ b/solution.py
@@ -456,7 +456,7 @@
     def totals(par, first, gamma_old, alpha_old):
         gamma, delta = gather(par, 2)
         ratio = jnp.where(first, 0.0, gamma / gamma_old)
-        alpha = gamma / (delta - ratio * gamma / alpha_old)
+        alpha = gamma / (delta - ratio * (gamma / alpha_old))
         return gamma, ratio, alpha
 
     for j in range(N):

time: 63 us -> 63 us (level)
  no operation moved by 1% of the time
where the time goes in v11:
time: 63 us; the launch traced here: 62.9 us
  Pallas kernels  61 us (97%)
  local copies, waits for them, and re-layouts  1.28 us (2%)
  between operations  0.64 us (1%)
    pallas_call x1, Pallas kernels, local(): pl.pallas_call(kernel, out_shape=(field, field), in_specs=[hbm] * 4, out_...  61 us
    unnamed x2, local copies, waits for them, and re-layouts  1.28 us

profile of v11, /device:TPU:1, one launch (start us, length us, event | category | flops | bytes accessed | tf_op | source)
XLA Modules:
  0.0 62.9 jit_solution(7418937888268217173)
XLA Ops:
  0.6 61.0 %solve.1 = (f32[1,6,32,128]{3,2,1,0:T(8,128)S(1)}, f32[1,6,32,128]{3,2,1,0:T(8,128)S(1)}) custom-call(s32[4,1,6]{2,1,0:T(1,128)} %links_in.1, f32[1,6,32,128]{3,2,1,0:T(8,128)} %load.1, bf16[24,128,128]{2,1,0:T(8,128)(2,1)} %bitcast.2, f32[6,1,128]{2,1,0:T(1,128)} %bitcast.3), custom_call_target="tpu_custom_call" | custom-call | tf_op jit(solution)/shard_map/solve/pallas_call | solution.py:527
  61.7 0.6 %copy.8 = f32[1,6,32,128]{3,2,1,0:T(8,128)} copy(f32[1,6,32,128]{3,2,1,0:T(8,128)S(1)} %get-tuple-element.4) | data formatting | bytes 196608
  62.3 0.6 %copy.9 = f32[1,6,32,128]{3,2,1,0:T(8,128)} copy(f32[1,6,32,128]{3,2,1,0:T(8,128)S(1)} %get-tuple-element.5) | data formatting | bytes 196608
